TPU v7x, 16 devices: a whole 2x2x2 slice. The times are simulated.
16 devices in a mesh: rep: 4 (over z, y), data: 4 (over x, core).
Axes of the slice: x: 2, y: 2, z: 2, core: 2. Of those that a mesh axis runs over, the one named last changes fastest.
Arguments:
- x: bfloat16 [2048, 5120], P(('rep', 'data')), parts along dimension 0
- adapter_id: int32 [2048], P(('rep', 'data')), parts along dimension 0
- dout: bfloat16 [2048, 5120], P(('rep', 'data')), parts along dimension 0
- w_gate: bfloat16 [5120, 13824], replicated
- w_up: bfloat16 [5120, 13824], replicated
- w_down: bfloat16 [13824, 5120], replicated
- a_gate: bfloat16 [64, 5120, 16], P('data')
- b_gate: bfloat16 [64, 16, 13824], P('data')
- a_up: bfloat16 [64, 5120, 16], P('data')
- b_up: bfloat16 [64, 16, 13824], P('data')
- a_down: bfloat16 [64, 13824, 16], P('data')
- b_down: bfloat16 [64, 16, 5120], P('data')
Outputs:
- output 1: bfloat16 [2048, 5120], P(('rep', 'data')), parts along dimension 0
- output 2: bfloat16 [2048, 5120], P(('rep', 'data')), parts along dimension 0
- output 3: float32 [256, 5120, 16], P(('rep', 'data')), parts along dimension 0
- output 4: float32 [256, 16, 13824], P(('rep', 'data')), parts along dimension 0
- output 5: float32 [256, 5120, 16], P(('rep', 'data')), parts along dimension 0
- output 6: float32 [256, 16, 13824], P(('rep', 'data')), parts along dimension 0
- output 7: float32 [256, 13824, 16], P(('rep', 'data')), parts along dimension 0
- output 8: float32 [256, 16, 5120], P(('rep', 'data')), parts along dimension 0
There are 4 independent parts. A program takes and returns all parts, laid end to end along the dimension named above; an argument that names none is the same for every part.
All inputs are finite; a program needn't handle non-finite values.
Results may differ from a plain program's by a relative error of at most 0.00763854.
Values are sent between devices in bfloat16 or wider.
A program may use at most 2 GiB of HBM per device.

v0:
```python
import jax
import jax.numpy as jnp
from jax import lax
from jax.sharding import PartitionSpec as P

value_a10 = 32


def grouped_rows(in_rows, weight_set, group_sizes, contract_dim):
    dim_numbers = lax.RaggedDotDimensionNumbers(
        dot_dimension_numbers=(([1], [contract_dim]), ([], [])),
        lhs_ragged_dimensions=[0],
        rhs_group_dimensions=[0],
    )
    return lax.ragged_dot_general(in_rows, weight_set, group_sizes, dim_numbers, preferred_element_type=jnp.float32)


def grouped_outer(left_rows, right_rows, group_sizes):
    dim_numbers = lax.RaggedDotDimensionNumbers(
        dot_dimension_numbers=(([0], [0]), ([], [])),
        lhs_ragged_dimensions=[0],
        rhs_group_dimensions=[],
    )
    return lax.ragged_dot_general(left_rows, right_rows, group_sizes, dim_numbers, preferred_element_type=jnp.float32)


def contract_last(left_rows, weight):
    return lax.dot_general(left_rows, weight, (((1,), (1,)), ((), ())), preferred_element_type=jnp.float32)


def solution(mesh):
    group_size = mesh.shape['data']
    tok_spec = P(('rep', 'data'), None)
    id_spec = P(('rep', 'data'))
    full_spec = P(None, None)
    own_spec = P('data', None, None)
    grad_spec = P(('rep', 'data'), None, None)

    def device_fn(x_loc, ids_loc, dy_loc, w_gate, w_up, w_down, a_gate, b_gate, a_up, b_up, a_down, b_down):
        tokens = x_loc.shape[0]
        n_local = a_gate.shape[0]
        array_b10 = value_a10 / a_gate.shape[2]
        capacity = ((3 * tokens + 8 * group_size - 1) // (8 * group_size)) * 8
        owner_dev = ids_loc // n_local
        by_owner = jnp.argsort(owner_dev, stable=True)
        position = jnp.argsort(by_owner, stable=True)
        counts = jnp.bincount(owner_dev, length=group_size)
        starts = jnp.cumsum(counts) - counts
        dest_slot = owner_dev * capacity + position - starts[owner_dev]
        slot_token = jnp.full((group_size * capacity,), tokens, jnp.int32).at[dest_slot].set(jnp.arange(tokens, dtype=jnp.int32))

        def pack_rows(in_rows):
            return jnp.take(in_rows, slot_token, axis=0, mode='fill', fill_value=0)

        arrived_ids = lax.all_to_all(pack_rows(ids_loc % n_local), 'data', 0, 0, tiled=True)
        sort_order = jnp.argsort(arrived_ids, stable=True)
        restore = jnp.argsort(sort_order, stable=True)
        group_sizes = jnp.bincount(arrived_ids, length=n_local).astype(jnp.int32)

        def to_owner(in_rows):
            arrived = lax.all_to_all(pack_rows(in_rows), 'data', 0, 0, tiled=True)
            return jnp.take(arrived, sort_order, axis=0)

        def to_source(owner_rows):
            returned = lax.all_to_all(jnp.take(owner_rows, restore, axis=0), 'data', 0, 0, tiled=True)
            return jnp.take(returned, dest_slot, axis=0)

        x_own = to_owner(x_loc)
        p_gate = grouped_rows(x_own, a_gate, group_sizes, 1).astype(jnp.bfloat16)
        p_up = grouped_rows(x_own, a_up, group_sizes, 1).astype(jnp.bfloat16)
        e_gate = to_source((array_b10 * grouped_rows(p_gate, b_gate, group_sizes, 1)).astype(jnp.bfloat16))
        e_up = to_source((array_b10 * grouped_rows(p_up, b_up, group_sizes, 1)).astype(jnp.bfloat16))
        gate_pre = jnp.dot(x_loc, w_gate, preferred_element_type=jnp.float32) + e_gate.astype(jnp.float32)
        up_pre = jnp.dot(x_loc, w_up, preferred_element_type=jnp.float32) + e_up.astype(jnp.float32)
        gate_sig = jax.nn.sigmoid(gate_pre)
        gate_act = gate_pre * gate_sig
        hidden = (gate_act * up_pre).astype(jnp.bfloat16)
        h_own = to_owner(hidden)
        p_down = grouped_rows(h_own, a_down, group_sizes, 1).astype(jnp.bfloat16)
        e_down = to_source((array_b10 * grouped_rows(p_down, b_down, group_sizes, 1)).astype(jnp.bfloat16))
        out_loc = (x_loc.astype(jnp.float32) + jnp.dot(hidden, w_down, preferred_element_type=jnp.float32) + e_down.astype(jnp.float32)).astype(jnp.bfloat16)
        dy_own = to_owner(dy_loc)
        q_down = (array_b10 * grouped_rows(dy_own, b_down, group_sizes, 2)).astype(jnp.bfloat16)
        value_a7 = to_source(grouped_rows(q_down, a_down, group_sizes, 2).astype(jnp.bfloat16))
        grad_b_down = array_b10 * grouped_outer(p_down, dy_own, group_sizes)
        grad_a_down = grouped_outer(h_own, q_down, group_sizes)
        d_hidden = contract_last(dy_loc, w_down) + value_a7.astype(jnp.float32)
        d_gate = (d_hidden * up_pre * gate_sig * (1.0 + gate_pre * (1.0 - gate_sig))).astype(jnp.bfloat16)
        d_up = (d_hidden * gate_act).astype(jnp.bfloat16)
        dg_own = to_owner(d_gate)
        du_own = to_owner(d_up)
        q_gate = (array_b10 * grouped_rows(dg_own, b_gate, group_sizes, 2)).astype(jnp.bfloat16)
        q_up = (array_b10 * grouped_rows(du_own, b_up, group_sizes, 2)).astype(jnp.bfloat16)
        array_b7 = to_source((grouped_rows(q_gate, a_gate, group_sizes, 2) + grouped_rows(q_up, a_up, group_sizes, 2)).astype(jnp.bfloat16))
        grad_a_gate = grouped_outer(x_own, q_gate, group_sizes)
        grad_b_gate = array_b10 * grouped_outer(p_gate, dg_own, group_sizes)
        grad_a_up = grouped_outer(x_own, q_up, group_sizes)
        grad_b_up = array_b10 * grouped_outer(p_up, du_own, group_sizes)
        dx_loc = (dy_loc.astype(jnp.float32) + contract_last(d_gate, w_gate) + contract_last(d_up, w_up) + array_b7.astype(jnp.float32)).astype(jnp.bfloat16)
        return out_loc, dx_loc, grad_a_gate, grad_b_gate, grad_a_up, grad_b_up, grad_a_down, grad_b_down

    return jax.shard_map(
        device_fn,
        mesh=mesh,
        in_specs=(tok_spec, id_spec, tok_spec, full_spec, full_spec, full_spec, own_spec, own_spec, own_spec, own_spec, own_spec, own_spec),
        out_specs=(tok_spec, tok_spec, grad_spec, grad_spec, grad_spec, grad_spec, grad_spec, grad_spec),
        check_vma=False,
    )
```

profile of v0, /device:TPU:1, one launch (start us, length us, event | category | flops | bytes accessed | tf_op | source)
XLA Modules:
  0.0 2250.5 jit_solution(462448334908285796)
XLA Ops:
  36.0 49.6 %all_to_all.129 = bf16[4,96,5120]{2,1,0:T(8,128)(2,1)} all-to-all(bf16[4,96,5120]{2,1,0:T(8,128)(2,1)} %bitcast.65), channel_id=1, replica_groups=mesh['rep'=4,'data'=4] {'data'}, dimensions={0} | all-to-all | bytes 7864320 | tf_op jit(solution)/shard_map/all_to_all | solution.py:61
  91.4 15.1 copy.39
  106.5 12.5 copy.40
  119.0 15.1 copy.42
  149.9 12.7 gather_fusion.2
  162.6 12.7 gather_fusion.12
  181.0 20.9 ragged-dot-none.17
  203.5 29.0 %ragged-dot-none.16 = f32[384,13824]{1,0:T(8,128)} custom-call(s32[1]{0:T(128)} %get-tuple-element.86, s32[17]{0:T(128)} %get-tuple-element.87, s32[18]{0:T(128)} %get-tuple-element.88, s32[18]{0:T(128)} %get-tuple-element.89, s32[1]{0:T(128)} %get-tuple-element.86, bf16[384,16]{1,0:T(8,128)(2,1)} %convert_element_type.70, bf16[16,16,13824]{2,1,0:T(8,128)(2,1)} %param.31), custom_call_target="tpu_custom_call" | custom-call | flops 169869312 | bytes 28323904 | tf_op jit(solution)/shard_map/ragged_dot_general/ragged-dot-none
  232.5 12.2 multiply_convert_fusion.1
  244.7 20.9 ragged-dot-none.15
  267.2 29.0 %ragged-dot-none.14 = f32[384,13824]{1,0:T(8,128)} custom-call(s32[1]{0:T(128)} %get-tuple-element.86, s32[17]{0:T(128)} %get-tuple-element.87, s32[18]{0:T(128)} %get-tuple-element.88, s32[18]{0:T(128)} %get-tuple-element.89, s32[1]{0:T(128)} %get-tuple-element.86, bf16[384,16]{1,0:T(8,128)(2,1)} %convert_element_type.73, bf16[16,16,13824]{2,1,0:T(8,128)(2,1)} %param.33), custom_call_target="tpu_custom_call" | custom-call | flops 169869312 | bytes 28323904 | tf_op jit(solution)/shard_map/ragged_dot_general/ragged-dot-none
  296.2 12.2 multiply_convert_fusion
  308.4 29.6 %gather_fusion.3 = bf16[384,13824]{1,0:T(8,128)(2,1)} fusion(bf16[384,13824]{1,0:T(8,128)(2,1)} %multiply_convert_fusion.1, s32[1024]{0:T(1024)S(1)} %pad_clamp_fusion.1), kind=kCustom, calls=%fused_computation.2.clone | custom fusion | bytes 21235200 | tf_op jit(solution)/shard_map/jit(_take)/gather | solution.py:65
  338.0 29.4 %gather_fusion.5 = bf16[384,13824]{1,0:T(8,128)(2,1)} fusion(bf16[384,13824]{1,0:T(8,128)(2,1)} %multiply_convert_fusion, s32[1024]{0:T(1024)S(1)} %pad_clamp_fusion.1), kind=kCustom, calls=%fused_computation.10.clone | custom fusion | bytes 21235200 | tf_op jit(solution)/shard_map/jit(_take)/gather | solution.py:65
  367.4 20.9 ragged-dot-none.11
  389.9 29.4 %ragged-dot-none.10 = f32[384,13824]{1,0:T(8,128)} custom-call(s32[1]{0:T(128)} %get-tuple-element.86, s32[17]{0:T(128)} %get-tuple-element.87, s32[18]{0:T(128)} %get-tuple-element.88, s32[18]{0:T(128)} %get-tuple-element.89, s32[1]{0:T(128)} %get-tuple-element.86, bf16[384,16]{1,0:T(8,128)(2,1)} %multiply_convert_fusion.8, bf16[16,16,13824]{2,1,0:T(8,128)(2,1)} %bitcast.61), custom_call_target="tpu_custom_call" | custom-call | flops 169869312 | bytes 28323904 | tf_op ragged-dot-none
  419.3 12.1 convert_element_type.83
  431.4 29.2 %gather_fusion.13 = bf16[384,13824]{1,0:T(8,128)(2,1)} fusion(bf16[384,13824]{1,0:T(8,128)(2,1)} %convert_element_type.83, s32[1024]{0:T(1024)S(1)} %pad_clamp_fusion.1), kind=kCustom, calls=%fused_computation.12.clone | custom fusion | bytes 21235200 | tf_op jit(solution)/shard_map/jit(_take)/gather | solution.py:65
  460.7 14.8 broadcast_select_fusion.6
  475.5 117.7 %all_to_all.130 = bf16[4,96,13824]{2,1,0:T(8,128)(2,1)} all-to-all(bf16[4,96,13824]{2,1,0:T(8,128)(2,1)S(1)} %bitcast.60), channel_id=1, replica_groups=mesh['rep'=4,'data'=4] {'data'}, dimensions={0} | all-to-all | bytes 21233664 | tf_op jit(solution)/shard_map/all_to_all | solution.py:65
  593.2 120.8 %all_to_all.131 = bf16[4,96,13824]{2,1,0:T(8,128)(2,1)} all-to-all(bf16[4,96,13824]{2,1,0:T(8,128)(2,1)S(1)} %bitcast.58), channel_id=1, replica_groups=mesh['rep'=4,'data'=4] {'data'}, dimensions={0} | all-to-all | bytes 21233664 | tf_op jit(solution)/shard_map/all_to_all | solution.py:65
  714.1 7.3 all-to-all-start.7
  721.4 13.1 gather_fusion.6
  734.5 13.3 gather_fusion.4
  747.7 89.4 %all-to-all-done.7 = bf16[4,96,13824]{2,1,0:T(8,128)(2,1)} async-done(((bf16[4,96,13824]{2,1,0:T(8,128)(2,1)}), bf16[4,96,13824]{2,1,0:T(8,128)(2,1)}, u32[]{:S(2)}, u32[]{:S(2)}) %all-to-all-start.7) | async-done | bytes 10616864 | tf_op jit(solution)/shard_map/all_to_all | solution.py:65
  837.1 13.2 gather_fusion.14
  850.3 49.7 %convolution_add_fusion.1 = f32[128,13824]{1,0:T(8,128)} fusion(bf16[128,5120]{1,0:T(8,128)(2,1)S(1)} %copy-done.5, bf16[5120,13824]{1,0:T(8,128)(2,1)} %param.28, bf16[128,13824]{1,0:T(8,128)(2,1)} %gather_fusion.6, pred[128]{0:T(512)(128)(4,1)S(1)} %copy-done.14), kind=kOutput, calls=%fused_computation.27 | convolution fusion | flops 18124701696 | bytes 153485440 | tf_op jit(solution)/shard_map/dot_general | solution.py:74
  900.0 49.3 %convolution_add_fusion.2 = f32[128,13824]{1,0:T(8,128)} fusion(bf16[128,5120]{1,0:T(8,128)(2,1)S(1)} %copy-done.5, bf16[5120,13824]{1,0:T(8,128)(2,1)} %param.27, bf16[128,13824]{1,0:T(8,128)(2,1)} %gather_fusion.4, pred[128]{0:T(512)(128)(4,1)S(1)} %copy-done.14), kind=kOutput, calls=%fused_computation.28 | convolution fusion | flops 18124701696 | bytes 153485440 | tf_op jit(solution)/shard_map/dot_general | solution.py:73
  949.2 60.5 %multiply_convert_fusion.3 = (bf16[128,13824]{1,0:T(8,128)(2,1)}, bf16[128,13824]{1,0:T(8,128)(2,1)}, bf16[128,13824]{1,0:T(8,128)(2,1)S(1)}) fusion(f32[128,13824]{1,0:T(8,128)} %convolution_add_fusion.2, f32[128,13824]{1,0:T(8,128)} %convolution_add_fusion.1, bf16[128,13824]{1,0:T(8,128)(2,1)} %gather_fusion.14, pred[128]{0:T(512)(128)(4,1)S(1)} %copy-done.14, ...), kind=kOutput, calls=%fused_computation.42 | convolution fusion | flops 18151243776 | bytes 171180160 | tf_op jit(solution)/shard_map/dot_general | solution.py:28
  1009.7 11.5 gather_fusion.7
  1021.3 26.6 %gather_fusion.15 = bf16[384,13824]{1,0:T(8,128)(2,1)} fusion(bf16[128,13824]{1,0:T(8,128)(2,1)} %get-tuple-element.127, s32[1024]{0:T(1024)S(1)} %copy-done.9), kind=kCustom, calls=%fused_computation.17.clone | custom fusion | bytes 21235200 | tf_op jit(solution)/shard_map/jit(_take)/gather | solution.py:53
  1047.9 11.7 gather_fusion.17
  1059.6 14.5 broadcast_select_fusion.3
  1074.1 120.6 %all_to_all.132 = bf16[4,96,13824]{2,1,0:T(8,128)(2,1)} all-to-all(bf16[4,96,13824]{2,1,0:T(8,128)(2,1)S(1)} %bitcast.59), channel_id=1, replica_groups=mesh['rep'=4,'data'=4] {'data'}, dimensions={0} | all-to-all | bytes 21233664 | tf_op jit(solution)/shard_map/all_to_all | solution.py:61
  1194.8 120.8 %all_to_all.133 = bf16[4,96,13824]{2,1,0:T(8,128)(2,1)} all-to-all(bf16[4,96,13824]{2,1,0:T(8,128)(2,1)S(1)} %bitcast.57), channel_id=1, replica_groups=mesh['rep'=4,'data'=4] {'data'}, dimensions={0} | all-to-all | bytes 21233664 | tf_op jit(solution)/shard_map/all_to_all | solution.py:61
  1322.6 39.0 %copy.44 = bf16[16,16,13824]{1,2,0:T(8,128)(2,1)} copy(bf16[16,16,13824]{2,1,0:T(8,128)(2,1)} %param.33) | data formatting | bytes 14155776 | tf_op args[9]
  1361.6 39.1 %copy.43 = bf16[16,16,13824]{1,2,0:T(8,128)(2,1)} copy(bf16[16,16,13824]{2,1,0:T(8,128)(2,1)} %param.31) | data formatting | bytes 14155776 | tf_op args[7]
  1400.6 39.1 %copy.41 = bf16[16,13824,16]{2,1,0:T(8,128)(2,1)} copy(bf16[16,13824,16]{1,2,0:T(8,128)(2,1)} %param.34) | data formatting | bytes 14155776 | tf_op args[10]
  1441.5 29.6 %gather_fusion.8 = bf16[384,13824]{1,0:T(8,128)(2,1)} fusion(bf16[384,13824]{1,0:T(8,128)(2,1)} %bitcast.47, s32[1024]{0:T(1024)S(1)} %copy-done.13), kind=kCustom, calls=%fused_computation.11.clone | custom fusion | bytes 21235200 | tf_op jit(solution)/shard_map/jit(_take)/gather | solution.py:62
  1471.2 29.4 %gather_fusion.16 = bf16[384,13824]{1,0:T(8,128)(2,1)} fusion(bf16[384,13824]{1,0:T(8,128)(2,1)} %bitcast.48, s32[1024]{0:T(1024)S(1)} %copy-done.13), kind=kCustom, calls=%fused_computation.13.clone | custom fusion | bytes 21235200 | tf_op jit(solution)/shard_map/jit(_take)/gather | solution.py:62
  1500.6 29.5 %gather_fusion.18 = bf16[384,13824]{1,0:T(8,128)(2,1)} fusion(bf16[384,13824]{1,0:T(8,128)(2,1)} %bitcast.28, s32[1024]{0:T(1024)S(1)} %copy-done.13), kind=kCustom, calls=%fused_computation.14.clone | custom fusion | bytes 21235200 | tf_op jit(solution)/shard_map/jit(_take)/gather | solution.py:62
  1530.0 20.5 broadcast_select_fusion
  1550.6 34.3 %ragged-dot-none.7 = f32[384,16]{1,0:T(8,128)} custom-call(s32[1]{0:T(128)} %get-tuple-element.86, s32[17]{0:T(128)} %get-tuple-element.87, s32[18]{0:T(128)} %get-tuple-element.88, s32[18]{0:T(128)} %get-tuple-element.89, s32[1]{0:T(128)} %get-tuple-element.86, bf16[384,13824]{1,0:T(8,128)(2,1)} %get-tuple-element.131, bf16[16,13824,16]{2,1,0:T(8,128)(2,1)} %bitcast.51), custom_call_target="tpu_custom_call" | custom-call | flops 169869312 | bytes 17719360 | tf_op ragged-dot-none
  1586.5 34.0 %ragged-dot-none.9 = f32[384,16]{1,0:T(8,128)} custom-call(s32[1]{0:T(128)} %get-tuple-element.86, s32[17]{0:T(128)} %get-tuple-element.87, s32[18]{0:T(128)} %get-tuple-element.88, s32[18]{0:T(128)} %get-tuple-element.89, s32[1]{0:T(128)} %get-tuple-element.86, bf16[384,13824]{1,0:T(8,128)(2,1)} %get-tuple-element.132, bf16[16,13824,16]{2,1,0:T(8,128)(2,1)} %bitcast.50), custom_call_target="tpu_custom_call" | custom-call | flops 169869312 | bytes 17719360 | tf_op ragged-dot-none
  1622.0 18.1 ragged-dot-none.6
  1640.1 18.0 ragged-dot-none.8
  1658.1 8.4 add_convert_fusion
  1666.5 12.7 gather_fusion.19
  1679.1 34.0 %ragged-dot-none.13 = f32[384,16]{1,0:T(8,128)} custom-call(s32[1]{0:T(128)} %get-tuple-element.86, s32[17]{0:T(128)} %get-tuple-element.87, s32[18]{0:T(128)} %get-tuple-element.88, s32[18]{0:T(128)} %get-tuple-element.89, s32[1]{0:T(128)} %get-tuple-element.86, bf16[384,13824]{1,0:T(8,128)(2,1)} %get-tuple-element.133, bf16[16,13824,16]{2,1,0:T(8,128)(2,1)} %copy.41), custom_call_target="tpu_custom_call" | custom-call | flops 169869312 | bytes 17719360 | tf_op jit(solution)/shard_map/ragged_dot_general/ragged-dot-none
  1714.7 18.1 ragged-dot-none.12
  1738.6 12.7 gather_fusion.9
  1762.3 56.2 %convolution_add_fusion.5 = f32[128,5120]{1,0:T(8,128)} fusion(bf16[128,13824]{1,0:T(8,128)(2,1)S(1)} %copy-done.3, bf16[5120,13824]{1,0:T(8,128)(2,1)} %param.27, bf16[128,5120]{1,0:T(8,128)(2,1)} %param.26), kind=kOutput, calls=%fused_computation.51 | convolution fusion | flops 18120704000 | bytes 149028864 | tf_op jit(solution)/shard_map/dot_general | solution.py:28
  1818.5 21.9 ragged-dot-none.2
  1840.4 21.9 ragged-dot-none.4
  1867.2 18.4 broadcast_multiply_fusion
  1885.6 61.4 %ragged-dot-none.1 = f32[16,13824,16]{2,1,0:T(8,128)} custom-call(s32[1]{0:T(128)} %get-tuple-element.42, s32[17]{0:T(128)} %get-tuple-element.43, s32[18]{0:T(128)} %get-tuple-element.44, s32[18]{0:T(128)} %get-tuple-element.45, s32[1]{0:T(128)} %get-tuple-element.42, bf16[384,13824]{1,0:T(8,128)(2,1)} %get-tuple-element.133, ...), custom_call_target="tpu_custom_call" | custom-call | flops 169869312 | bytes 24784960 | tf_op jit(solution)/shard_map/ragged_dot_general/ragged-dot-none
  1947.0 61.1 %copy.47 = f32[16,13824,16]{1,2,0:T(8,128)} copy(f32[16,13824,16]{2,1,0:T(8,128)} %ragged-dot-none.1) | data formatting | bytes 28311552
  2008.1 29.5 %ragged-dot-none.3 = f32[16,5120,16]{2,1,0:T(8,128)} custom-call(s32[1]{0:T(128)} %get-tuple-element.42, s32[17]{0:T(128)} %get-tuple-element.43, s32[18]{0:T(128)} %get-tuple-element.44, s32[18]{0:T(128)} %get-tuple-element.45, s32[1]{0:T(128)} %get-tuple-element.42, bf16[384,5120]{1,0:T(8,128)(2,1)} %get-tuple-element.141, ...), custom_call_target="tpu_custom_call" | custom-call | flops 62914560 | bytes 9187392 | tf_op jit(solution)/shard_map/ragged_dot_general/ragged-dot-none
  2037.7 23.3 %copy.46 = f32[16,5120,16]{1,2,0:T(8,128)} copy(f32[16,5120,16]{2,1,0:T(8,128)} %ragged-dot-none.3) | data formatting | bytes 10485760
  2061.0 29.5 %ragged-dot-none.5 = f32[16,5120,16]{2,1,0:T(8,128)} custom-call(s32[1]{0:T(128)} %get-tuple-element.42, s32[17]{0:T(128)} %get-tuple-element.43, s32[18]{0:T(128)} %get-tuple-element.44, s32[18]{0:T(128)} %get-tuple-element.45, s32[1]{0:T(128)} %get-tuple-element.42, bf16[384,5120]{1,0:T(8,128)(2,1)} %get-tuple-element.141, ...), custom_call_target="tpu_custom_call" | custom-call | flops 62914560 | bytes 9187392 | tf_op jit(solution)/shard_map/ragged_dot_general/ragged-dot-none
  2090.5 23.3 %copy.45 = f32[16,5120,16]{1,2,0:T(8,128)} copy(f32[16,5120,16]{2,1,0:T(8,128)} %ragged-dot-none.5) | data formatting | bytes 10485760
  2113.8 15.1 ragged-dot-none
  2147.3 47.5 %fusion.3 = bf16[128,5120]{1,0:T(8,128)(2,1)} fusion(bf16[128,13824]{1,0:T(8,128)(2,1)S(1)} %copy-done.1, bf16[13824,5120]{1,0:T(8,128)(2,1)} %param.29, bf16[128,5120]{1,0:T(8,128)(2,1)} %param.24, bf16[128,5120]{1,0:T(8,128)(2,1)} %gather_fusion.10, pred[128]{0:T(512)(128)(4,1)S(1)} %copy-done.15), kind=kOutput, calls=%fused_computation.52 | convolution fusion | flops 18123325440 | bytes 149028992 | tf_op jit(solution)/shard_map/dot_general | solution.py:81
  2194.7 55.4 %fusion.4 = bf16[128,5120]{1,0:T(8,128)(2,1)} fusion(f32[128,5120]{1,0:T(8,128)} %convolution_add_fusion.5, bf16[128,13824]{1,0:T(8,128)(2,1)} %get-tuple-element.126, bf16[5120,13824]{1,0:T(8,128)(2,1)} %param.28, bf16[128,5120]{1,0:T(8,128)(2,1)} %gather_fusion.20, pred[128]{0:T(512)(128)(4,1)S(1)} %copy-done.15), kind=kOutput, calls=%fused_computation.53 | convolution fusion | flops 18122670080 | bytes 150339712 | tf_op jit(solution)/shard_map/dot_general | solution.py:28
  (112 shorter events, 121.0 us)
Async XLA Ops:
  0.6 20.4 copy-start.4
  11.8 0.5 copy-start.23
  13.3 12.3 copy-start.8
  16.1 14.2 copy-start.21
  16.7 19.2 all-to-all-start.1
  21.0 4.6 copy-start.6
  85.5 77.0 %all-to-all-start.6 = ((bf16[4,96,5120]{2,1,0:T(8,128)(2,1)}), bf16[4,96,5120]{2,1,0:T(8,128)(2,1)}, u32[]{:S(2)}, u32[]{:S(2)}) async-start(bf16[4,96,5120]{2,1,0:T(8,128)(2,1)} %bitcast.62), calls=%async_computation.6 | async-start | bytes 7864320 | tf_op jit(solution)/shard_map/all_to_all | solution.py:61
  91.4 15.1 copy-start.7
  149.3 13.3 copy-start.12
  149.4 282.1 %copy-start.10 = (s32[1024]{0:T(1024)}, s32[1024]{0:T(1024)S(1)}, u32[]{:S(2)}) copy-start(s32[1024]{0:T(1024)S(1)} %pad_clamp_fusion.1) | copy-start | bytes 12292
  149.4 25.9 %copy-start.19 = (pred[384]{0:T(512)(128)(4,1)}, pred[384]{0:T(512)(128)(4,1)S(1)}, u32[]{:S(2)}) copy-start(pred[384]{0:T(512)(128)(4,1)S(1)} %compare_and_fusion.2) | copy-start | bytes 1156
  431.4 29.2 %copy-start.17 = (pred[384]{0:T(512)(128)(4,1)S(1)}, pred[384]{0:T(512)(128)(4,1)}, u32[]{:S(2)}) copy-start(pred[384]{0:T(512)(128)(4,1)} %compare_and_fusion.1) | copy-start | bytes 1156
  714.1 7.3 copy-start.24
  714.1 123.0 %all-to-all-start.7 = ((bf16[4,96,13824]{2,1,0:T(8,128)(2,1)}), bf16[4,96,13824]{2,1,0:T(8,128)(2,1)}, u32[]{:S(2)}, u32[]{:S(2)}) async-start(bf16[4,96,13824]{2,1,0:T(8,128)(2,1)} %bitcast.56), calls=%async_computation.7 | async-start | bytes 21233664 | tf_op jit(solution)/shard_map/all_to_all | solution.py:65
  721.4 115.7 %copy-start.16 = (s32[1024]{0:T(1024)}, s32[1024]{0:T(1024)S(1)}, u32[]{:S(2)}) copy-start(s32[1024]{0:T(1024)S(1)} %pad_clamp_fusion) | copy-start | bytes 12292
  837.1 13.2 copy-start.5
  837.1 13.2 copy-start.14
  949.2 60.5 %copy-start.9 = (s32[1024]{0:T(1024)S(1)}, s32[1024]{0:T(1024)}, u32[]{:S(2)}) copy-start(s32[1024]{0:T(1024)} %copy-done.8) | copy-start | bytes 12292
  1009.7 11.5 copy-start
  1021.3 26.6 %copy-start.2 = (bf16[128,13824]{1,0:T(8,128)(2,1)S(1)}, bf16[128,13824]{1,0:T(8,128)(2,1)}, u32[]{:S(2)}) copy-start(bf16[128,13824]{1,0:T(8,128)(2,1)} %get-tuple-element.126) | copy-start | bytes 10616836
  1047.9 11.7 copy-start.22
  1315.6 185.0 %all-to-all-start.9 = ((bf16[4,96,13824]{2,1,0:T(8,128)(2,1)}), bf16[4,96,13824]{2,1,0:T(8,128)(2,1)}, u32[]{:S(2)}, u32[]{:S(2)}) async-start(bf16[4,96,13824]{2,1,0:T(8,128)(2,1)} %bitcast.55), calls=%async_computation.9 | async-start | bytes 21233664 | tf_op jit(solution)/shard_map/all_to_all | solution.py:61
  1400.6 40.9 %copy-start.13 = (s32[1024]{0:T(1024)S(1)}, s32[1024]{0:T(1024)}, u32[]{:S(2)}) copy-start(s32[1024]{0:T(1024)} %copy-done.12) | copy-start | bytes 12292
  1500.6 29.5 %copy-start.20 = (pred[384]{0:T(512)(128)(4,1)S(1)}, pred[384]{0:T(512)(128)(4,1)}, u32[]{:S(2)}) copy-start(pred[384]{0:T(512)(128)(4,1)} %copy-done.19) | copy-start | bytes 1156
  1658.1 8.4 copy-start.11
  1738.6 12.7 copy-start.18
  1757.0 5.3 copy-start.3
  1757.0 105.4 %all-to-all-start.10 = ((bf16[4,96,5120]{2,1,0:T(8,128)(2,1)}), bf16[4,96,5120]{2,1,0:T(8,128)(2,1)}, u32[]{:S(2)}, u32[]{:S(2)}) async-start(bf16[4,96,5120]{2,1,0:T(8,128)(2,1)} %bitcast.64), calls=%async_computation.10 | async-start | bytes 7864320 | tf_op jit(solution)/shard_map/all_to_all | solution.py:65
  1862.4 278.3 %all-to-all-start.5 = ((bf16[4,96,5120]{2,1,0:T(8,128)(2,1)}), bf16[4,96,5120]{2,1,0:T(8,128)(2,1)}, u32[]{:S(2)}, u32[]{:S(2)}) async-start(bf16[4,96,5120]{2,1,0:T(8,128)(2,1)} %bitcast.63), calls=%async_computation.5 | async-start | bytes 7864320 | tf_op jit(solution)/shard_map/all_to_all | solution.py:65
  2140.7 6.6 copy-start.1
  2140.7 6.6 copy-start.15
where the time goes:
time: 2270 us; the launch traced here: 2250 us
  local copies, waits for them, and re-layouts  613 us (27%)
  blocking collectives  530 us (23%)
  Pallas kernels  490 us (22%)
  matrix products  318 us (14%)
  other arithmetic  175 us (8%)
  waiting for transfers between devices  89.4 us (4%)
  starting transfers between devices  34.5 us (2%)
    another operation x12, Pallas kernels  331 us
    all_to_all x3, blocking collectives, to_owner(): arrived = lax.all_to_all(pack_rows(in_rows), 'data', 0, 0, tiled=True)  291 us
    unnamed x59, local copies, waits for them, and re-layouts  268 us
    all_to_all x2, blocking collectives, to_source(): lax.all_to_all(jnp.take(owner_rows, restore, axis=0), 'data', 0, 0, tiled...  239 us
    dot_general x3, matrix products, contract_last(): lax.dot_general(left_rows, weight, (((1,), (1,)), ((), ())), preferred_el...  172 us
    unnamed x8, Pallas kernels  158 us
    gather x5, local copies, waits for them, and re-layouts, to_owner(): return jnp.take(arrived, sort_order, axis=0)  114 us
    gather x5, local copies, waits for them, and re-layouts, to_source(): jnp.take(owner_rows, restore, axis=0)  114 us
  transfers between devices with their start and end apart: 6, of which 1 were waited for; matrix products, arithmetic and copies ran while one was open for 21% of the time, Pallas kernels for 8%

commit v1 on v0

v1 whole, which is shorter than its diff:
```python
import functools

import jax
import jax.numpy as jnp
from jax import lax
from jax.experimental import pallas as pl
from jax.experimental.pallas import tpu as pltpu
from jax.sharding import PartitionSpec as P


ALPHA = 32
CORE_SWAP = [(0, 1), (1, 0), (2, 3), (3, 2)]
CHIP_SWAP = [(0, 2), (2, 0), (1, 3), (3, 1)]
F32, BF16 = jnp.float32, jnp.bfloat16


VMEM_BYTES = 64000 * 1024
SHORT = 216


def dot_nn(a, b):
    return lax.dot_general(a, b, (((1,), (0,)), ((), ())), preferred_element_type=F32)


def dot_nt(a, b):
    return lax.dot_general(a, b, (((1,), (1,)), ((), ())), preferred_element_type=F32)


def call(kernel, grid, in_specs, out_specs, out_shape, scratch, flops, nbytes, aliases={}):
    return pl.pallas_call(
        kernel,
        grid_spec=pltpu.PrefetchScalarGridSpec(
            num_scalar_prefetch=1, grid=grid, in_specs=in_specs, out_specs=out_specs, scratch_shapes=scratch),
        out_shape=out_shape,
        input_output_aliases=aliases,
        compiler_params=pltpu.CompilerParams(
            dimension_semantics=('arbitrary',) * len(grid), vmem_limit_bytes=VMEM_BYTES),
        cost_estimate=pl.CostEstimate(flops=int(flops), bytes_accessed=int(nbytes), transcendentals=0),
    )


def both_forms(info_ref, section, body):
    @pl.when(info_ref[2] == 1)
    def _():
        body(SHORT)

    @pl.when(info_ref[2] == 0)
    def _():
        body(section)


def turned(tile, off):
    parts = [tile[off:2 * off], tile[:off]]
    if 2 * off < tile.shape[0]:
        parts.append(tile[2 * off:])
    return jnp.concatenate(parts, axis=0)


def pack_kernel(factor, width, rank, n_mat, info_ref, local_ref, ids_ref, r0_ref, r1_ref, r2_ref, r3_ref, *refs):
    mats, (packed_ref, p_ref, turned_ref, pt_ref, turned_t_ref, acc, sel) = refs[:n_mat], refs[n_mat:]
    step = pl.program_id(0)
    slots = packed_ref.shape[0]
    section = slots // 2

    @pl.when(step == 0)
    def _():
        acc[...] = jnp.zeros_like(acc)
        row = lax.broadcasted_iota(jnp.int32, (section, section), 0)
        for a in range(2):
            sel[a] = jnp.where(row == local_ref[a:a + 1, :], 1.0, 0.0).astype(BF16)

    mine = dot_nn(sel[0], jnp.concatenate([r0_ref[...], r1_ref[...]], axis=0))
    sib = dot_nn(sel[1], jnp.concatenate([r2_ref[...], r3_ref[...]], axis=0))

    def place(off):
        parts = [mine[:off], sib[:off]]
        if off < section:
            parts.append(jnp.zeros((slots - 2 * off, mine.shape[1]), F32))
        packed_ref[...] = jnp.concatenate(parts, axis=0).astype(BF16)

    both_forms(info_ref, section, place)
    v = packed_ref[...]
    for k, mat in enumerate(mats):
        acc[:, k * width:(k + 1) * width] += dot_nt(v, mat[...])

    @pl.when(step == pl.num_programs(0) - 1)
    def _():
        owner = ids_ref[...] - info_ref[0] * (width // rank)
        col = lax.broadcasted_iota(jnp.int32, (slots, width), 1) // rank
        keep = owner == col
        for k in range(n_mat):
            cols = slice(k * width, (k + 1) * width)
            acc[:, cols] = jnp.where(keep, acc[:, cols] * factor, 0.0)
        p_ref[...] = acc[...].astype(BF16)
        pt_ref[...] = acc[...].T.astype(BF16)

        def emit(off):
            other = turned(acc[...], off)
            turned_ref[...] = other.astype(BF16)
            turned_t_ref[...] = other.T.astype(BF16)

        both_forms(info_ref, section, emit)


def dh_kernel(info_ref, dy_ref, wd_ref, qo_ref, qs_ref, ado_ref, ads_ref, dh_ref):
    def body(off):
        m = 2 * off
        eh = (dot_nn(qo_ref[:m], ado_ref[...]) + dot_nn(qs_ref[:m], ads_ref[...])).astype(BF16)
        dh_ref[:m] = dot_nt(dy_ref[:m], wd_ref[...]) + eh.astype(F32)

    both_forms(info_ref, dy_ref.shape[0] // 2, body)


def hidden_kernel(scale, width, info_ref, x_ref, dh_ref, wg_ref, wu_ref, po_ref, ps_ref,
                  bgo_ref, bgs_ref, buo_ref, bus_ref, ado_ref, ads_ref, pt_ref, qt_ref,
                  h3_ref, qo_ref, qs_ref, gbg_ref, gbu_ref, gad_ref):
    step = pl.program_id(0)
    slots = x_ref.shape[0]

    @pl.when(step == 0)
    def _():
        qo_ref[...] = jnp.zeros_like(qo_ref)
        qs_ref[...] = jnp.zeros_like(qs_ref)

    def body(off):
        m = 2 * off

        def rank_side(k, o_ref, s_ref):
            cols = slice(k * width, (k + 1) * width)
            return dot_nn(po_ref[:m, cols], o_ref[...]) + dot_nn(ps_ref[:m, cols], s_ref[...])

        eg = (scale * rank_side(0, bgo_ref, bgs_ref)).astype(BF16)
        eu = (scale * rank_side(1, buo_ref, bus_ref)).astype(BF16)
        gate = dot_nn(x_ref[:m], wg_ref[...]) + eg.astype(F32)
        up = dot_nn(x_ref[:m], wu_ref[...]) + eu.astype(F32)
        dh = dh_ref[:m]
        sig = jax.nn.sigmoid(gate)
        act = gate * sig
        h = (act * up).astype(BF16)
        dg = (dh * up * sig * (1.0 + gate * (1.0 - sig))).astype(BF16)
        du = (dh * act).astype(BF16)
        for k, (val, o_ref, s_ref) in enumerate(((h, ado_ref, ads_ref), (dg, bgo_ref, bgs_ref), (du, buo_ref, bus_ref))):
            cols = slice(k * width, (k + 1) * width)
            h3_ref[k, :m] = val
            if m < slots:
                h3_ref[k, m:] = jnp.zeros((slots - m, val.shape[1]), BF16)
            qo_ref[:m, cols] += dot_nt(val, o_ref[...])
            qs_ref[:m, cols] += dot_nt(val, s_ref[...])

        @pl.when(step == pl.num_programs(0) - 1)
        def _():
            qs_ref[...] = turned(qs_ref[...], off)

    both_forms(info_ref, slots // 2, body)
    wide_grads(scale, width, h3_ref, pt_ref, qt_ref, gbg_ref, gbu_ref, gad_ref)


def wide_grads(scale, width, v_ref, pt_ref, qt_ref, gbg_ref, gbu_ref, gad_ref):
    gbg_ref[...] = scale * dot_nn(pt_ref[:width, :], v_ref[1])
    gbu_ref[...] = scale * dot_nn(pt_ref[width:, :], v_ref[2])
    gad_ref[...] = dot_nn(qt_ref[...], v_ref[0])


def rank_kernel(scale, width, rank, info_ref, ids_ref, own_ref, got_ref, q_ref, qt_ref):
    owner = ids_ref[...] - info_ref[0] * (width // rank)
    keep = owner == lax.broadcasted_iota(jnp.int32, (own_ref.shape[0], width), 1) // rank
    for k in range(3):
        cols = slice(k * width, (k + 1) * width)
        total = own_ref[:, cols] + got_ref[:, cols]
        total = jnp.where(keep, total * scale if k else total, 0.0)
        q_ref[:, cols] = total.astype(BF16)
        qt_ref[cols, :] = total.T.astype(BF16)


def finish_kernel(info_ref, local_ref, mine_ref, got_ref, base_ref, near_ref, far_ref):
    section = mine_ref.shape[0]
    val = (base_ref[...].astype(F32) + mine_ref[...] + got_ref[...]).astype(BF16)
    sel = jnp.where(local_ref[...] == lax.broadcasted_iota(jnp.int32, (section, section), 1), 1.0, 0.0).astype(BF16)
    rows = dot_nn(sel, val).astype(BF16)
    near_ref[...] = rows[:section // 2]
    far_ref[...] = rows[section // 2:]


def split_store(tile, off, mine_ref, sib_ref):
    mine_ref[:off] = tile[:off]
    sib_ref[:off] = tile[off:]
    if off < mine_ref.shape[0]:
        rest = jnp.zeros((mine_ref.shape[0] - off, tile.shape[1]), F32)
        mine_ref[off:] = rest
        sib_ref[off:] = rest


def dx_kernel(width, info_ref, dg_ref, du_ref, wg_ref, wu_ref, q_ref, ag_ref, au_ref, mine_ref, sib_ref):
    def body(off):
        m = 2 * off
        lora = (dot_nn(q_ref[:m, width:2 * width], ag_ref[...]) + dot_nn(q_ref[:m, 2 * width:], au_ref[...])).astype(BF16)
        tile = dot_nt(dg_ref[0, :m], wg_ref[...]) + dot_nt(du_ref[0, :m], wu_ref[...]) + lora.astype(F32)
        split_store(tile, off, mine_ref, sib_ref)

    both_forms(info_ref, mine_ref.shape[0], body)


def out_kernel(scale, width, info_ref, h_ref, wd_ref, q_ref, bd_ref, mine_ref, sib_ref):
    def body(off):
        m = 2 * off
        lora = (scale * dot_nn(q_ref[:m, :width], bd_ref[...])).astype(BF16)
        tile = dot_nn(h_ref[0, :m], wd_ref[...]) + lora.astype(F32)
        split_store(tile, off, mine_ref, sib_ref)

    both_forms(info_ref, mine_ref.shape[0], body)


def wide_grad_kernel(scale, width, info_ref, v_ref, pt_ref, qt_ref, gbg_in, gbu_in, gad_in, gbg_ref, gbu_ref, gad_ref):
    wide_grads(scale, width, v_ref, pt_ref, qt_ref, gbg_ref, gbu_ref, gad_ref)


def model_grad_kernel(scale, width, info_ref, x_ref, d_ref, qt_ref, gbd_ref, gag_ref, gau_ref):
    gbd_ref[...] = scale * dot_nn(qt_ref[:width, :], d_ref[...])
    gag_ref[...] = dot_nn(qt_ref[width:2 * width, :], x_ref[...])
    gau_ref[...] = dot_nn(qt_ref[2 * width:, :], x_ref[...])


def solution(mesh):
    tok_spec = P(('rep', 'data'), None)
    id_spec = P(('rep', 'data'))
    full_spec = P(None, None)
    own_spec = P('data', None, None)
    grad_spec = P(('rep', 'data'), None, None)

    def layer(x_loc, ids_loc, dy_loc, w_gate, w_up, w_down, a_gate, b_gate, a_up, b_up, a_down, b_down):
        toks, dim = x_loc.shape
        hid = w_gate.shape[1]
        n_local, rank = a_gate.shape[0], a_gate.shape[2]
        width = n_local * rank
        scale = ALPHA / rank
        fh = hid // 2
        section = 2 * toks
        slots = 2 * section
        me = lax.axis_index('data')
        core = me % 2
        chip = me // 2
        tie = lax.optimization_barrier

        def core_swap(v):
            return lax.ppermute(v, 'data', CORE_SWAP)

        def chip_swap(v):
            return lax.ppermute(v, 'data', CHIP_SWAP)

        ag = a_gate.transpose(0, 2, 1).reshape(width, dim)
        au = a_up.transpose(0, 2, 1).reshape(width, dim)
        bd = b_down.reshape(width, dim)
        bg = b_gate.reshape(width, hid)
        bu = b_up.reshape(width, hid)
        ad = a_down.transpose(0, 2, 1).reshape(width, hid)

        ids_mine = jnp.concatenate([ids_loc, chip_swap(ids_loc)])
        dy_send, ids_mine = tie((dy_loc, ids_mine))
        dy1 = chip_swap(dy_send)
        dy2, x2 = core_swap(dy_send), core_swap(x_loc)
        late_core, x2 = tie((core, x2))
        ids = jnp.concatenate([ids_mine, core_swap(ids_mine)])
        here = (ids // (2 * n_local) == chip).reshape(2, section)
        before = jnp.arange(section)[:, None] <= jnp.arange(section)[None, :]
        ends = jnp.dot(here.astype(F32), before.astype(F32)).astype(jnp.int32)
        short = jnp.max(ends) <= SHORT if SHORT < section else jnp.bool_(False)
        local = jnp.where(here, ends - 1, -1)
        place = local + jnp.where(short, SHORT, section) * jnp.arange(2, dtype=jnp.int32)[:, None]
        slot = jnp.where(here, place, -1).reshape(slots)
        hit = slot[None, :] == jnp.arange(slots, dtype=jnp.int32)[:, None]
        ids_slot = jnp.sum(jnp.where(hit, ids[None, :] + 1, 0), axis=1, dtype=jnp.int32) - 1
        info = jnp.stack([me, core, short.astype(jnp.int32)]).astype(jnp.int32)

        def for_sibling(v):
            return core_swap(lax.dynamic_slice_in_dim(v, (1 - late_core) * fh, fh, 1))

        ad_s, bg_s, bu_s = for_sibling(ad), for_sibling(bg), for_sibling(bu)
        dy1, ad_s, bg_s, bu_s, local, ids_slot, info = tie((dy1, ad_s, bg_s, bu_s, local, ids_slot, info))
        x_send, dy1 = tie((x_loc, dy1))
        x1 = chip_swap(x_send)
        dy3 = core_swap(dy1)

        one = dict(pipeline_mode=pl.Buffered(1))
        kt = 1024
        const = lambda *shape: pl.BlockSpec(shape, lambda i, s: (0,) * len(shape))
        vec = lambda r: pl.BlockSpec((r, kt), lambda i, s: (0, i))

        def pack(factor, rows, mats):
            n = len(mats)
            return call(
                functools.partial(pack_kernel, factor, width, rank, n), (dim // kt,),
                [const(2, section), const(slots, 1)] + [vec(toks)] * 4 + [vec(width)] * n,
                [vec(slots)] + [const(slots, n * width)] * 2 + [const(n * width, slots)] * 2,
                [jax.ShapeDtypeStruct((slots, dim), BF16)] + [jax.ShapeDtypeStruct((slots, n * width), BF16)] * 2
                + [jax.ShapeDtypeStruct((n * width, slots), BF16)] * 2,
                [pltpu.VMEM((slots, n * width), F32), pltpu.VMEM((2, section, section), BF16)],
                slots * dim * slots + 2 * n * slots * width * dim, 4 * slots * dim,
            )(info, local, ids_slot[:, None], *rows, *mats)

        dc, q_own, q_turned, qt_own, qt_turned = pack(scale, (dy_loc, dy1, dy2, dy3), (bd,))
        const1 = lambda *shape: pl.BlockSpec(shape, lambda i, s: (0,) * len(shape), **one)

        def tiles(ft):
            nf = fh // ft
            return (nf, pl.BlockSpec((width, ft), lambda i, s: (0, s[1] * nf + i)), pl.BlockSpec((width, ft), lambda i, s: (0, i)),
                    pl.BlockSpec((dim, ft), lambda i, s: (0, s[1] * nf + i)), pl.BlockSpec((ft, dim), lambda i, s: (s[1] * nf + i, 0)))

        ft = 768
        nf, own_tile, sib_tile, w_col, w_row = tiles(ft)
        dh = call(
            dh_kernel, (nf,),
            [const1(slots, dim), w_row, const1(slots, width), const1(slots, width), own_tile, sib_tile],
            pl.BlockSpec((slots, ft), lambda i, s: (0, i)), jax.ShapeDtypeStruct((slots, fh), F32),
            [], 2 * slots * dim * fh * 1.2, 2 * dim * fh,
        )(info, dc, w_down, q_own, core_swap(q_turned), ad, ad_s)
        x1, dh = tie((x1, dh))
        x3 = core_swap(x1)
        xc, p_own, p_turned, pt_own, pt_turned = pack(1.0, (x_loc, x1, x2, x3), (ag, au))
        ft = 256
        nf, own_tile, sib_tile, w_col, w_row = tiles(ft)
        g_out = pl.BlockSpec((width, ft), lambda i, s: (0, s[1] * nf + i))
        h3, qo, qs, gbg, gbu, gad = call(
            functools.partial(hidden_kernel, scale, width), (nf,),
            [const1(slots, dim), pl.BlockSpec((slots, ft), lambda i, s: (0, i)), w_col, w_col,
             const1(slots, 2 * width), const1(slots, 2 * width),
             own_tile, sib_tile, own_tile, sib_tile, own_tile, sib_tile, const1(2 * width, slots), const1(width, slots)],
            [pl.BlockSpec((3, slots, ft), lambda i, s: (0, 0, i)), const(slots, 3 * width), const(slots, 3 * width)] + [g_out] * 3,
            [jax.ShapeDtypeStruct((3, slots, fh), BF16)] + [jax.ShapeDtypeStruct((slots, 3 * width), F32)] * 2
            + [jax.ShapeDtypeStruct((width, hid), F32)] * 3,
            [], 4 * slots * dim * fh * 1.2, 4 * dim * fh,
        )(info, xc, dh, w_gate, w_up, p_own, core_swap(p_turned), bg, bg_s, bu, bu_s, ad, ad_s, pt_own, qt_own)

        q, qt = call(
            functools.partial(rank_kernel, scale, width, rank), (1,),
            [const(slots, 1), const(slots, 3 * width), const(slots, 3 * width)],
            [const(slots, 3 * width), const(3 * width, slots)],
            [jax.ShapeDtypeStruct((slots, 3 * width), BF16), jax.ShapeDtypeStruct((3 * width, slots), BF16)], [],
            1000000, 12 * slots * width,
        )(info, ids_slot[:, None], qo, core_swap(qs))
        h3_late, q = tie((h3, q))
        h3_rec = core_swap(h3_late)

        dt = 512
        q_spec = const1(slots, 3 * width)

        def plane(k):
            return pl.BlockSpec((1, slots, fh), lambda j, s: (k, 0, 0), **one)

        def dx_side(info):
            w_spec = pl.BlockSpec((dt, fh), lambda j, s: (j, s[1]))
            l_spec = pl.BlockSpec((width, dt), lambda j, s: (0, j))
            o_spec = pl.BlockSpec((section, dt), lambda j, s: (0, j))
            return call(
                functools.partial(dx_kernel, width), (dim // dt,),
                [plane(1), plane(2), w_spec, w_spec, q_spec, l_spec, l_spec], [o_spec, o_spec],
                [jax.ShapeDtypeStruct((section, dim), F32)] * 2, [],
                4 * slots * dim * fh, 4 * dim * fh,
            )(info, h3, h3, w_gate, w_up, q, ag, au)

        def out_side(info, first, count):
            w_spec = pl.BlockSpec((fh, dt), lambda j, s: (s[1], first + j))
            l_spec = pl.BlockSpec((width, dt), lambda j, s: (0, first + j))
            o_spec = pl.BlockSpec((section, dt), lambda j, s: (0, j))
            return call(
                functools.partial(out_kernel, scale, width), (count,),
                [plane(0), w_spec, q_spec, l_spec], [o_spec, o_spec],
                [jax.ShapeDtypeStruct((section, count * dt), F32)] * 2, [],
                2 * slots * count * dt * fh, 2 * count * dt * fh,
            )(info, h3, w_down, q, bd)

        def finish(mine, got, base, first):
            ct = 1280
            wide = mine.shape[1]
            cols = lambda r: pl.BlockSpec((r, ct), lambda i, s: (0, i))
            return call(
                finish_kernel, (wide // ct,),
                [const(section, 1), cols(section), cols(section), pl.BlockSpec((section, ct), lambda i, s: (0, first // ct + i))],
                [cols(toks), cols(toks)],
                [jax.ShapeDtypeStruct((toks, wide), BF16)] * 2, [],
                2 * section * section * wide, 12 * section * wide,
            )(info, local[0][:, None], mine, got, base)

        n_out = dim // dt // 2
        cut = n_out * dt
        dx_mine, dx_sib = dx_side(info)
        info_a, dx_sib = tie((info, dx_sib))
        dx_got = core_swap(dx_sib)
        a_mine, a_sib = out_side(info_a, 0, n_out)
        dx_got, a_sib = tie((dx_got, a_sib))
        dx_near, dx_far = finish(dx_mine, dx_got, dc, 0)
        a_got = core_swap(a_sib)
        info_b, dx_far = tie((info, dx_far))
        dx_back = chip_swap(dx_far)
        b_mine, b_sib = out_side(info_b, n_out, n_out)
        a_got, b_sib = tie((a_got, b_sib))
        a_near, a_far = finish(a_mine, a_got, xc, 0)
        b_got = core_swap(b_sib)
        info_c, a_far = tie((info, a_far))
        a_back = chip_swap(a_far)

        mt = 640
        m_spec = lambda r: pl.BlockSpec((r, mt), lambda i, s: (0, i))
        gbd, gag, gau = call(
            functools.partial(model_grad_kernel, scale, width), (dim // mt,),
            [m_spec(slots)] * 2 + [const(3 * width, slots)], [m_spec(width)] * 3,
            [jax.ShapeDtypeStruct((width, dim), F32)] * 3, [],
            6 * slots * width * dim, 12 * width * dim,
        )(info_c, xc, dc, qt)
        b_got, gbd = tie((b_got, gbd))
        b_near, b_far = finish(b_mine, b_got, xc, cut)
        info_d, b_far = tie((info, b_far))
        b_back = chip_swap(b_far)

        gt = 768
        n_half = fh // gt
        g_rest = pl.BlockSpec((width, gt), lambda i, s: (0, (1 - s[1]) * n_half + i))
        gbg, gbu, gad = call(
            functools.partial(wide_grad_kernel, scale, width), (n_half,),
            [pl.BlockSpec((3, slots, gt), lambda i, s: (0, 0, i)), const(2 * width, slots), const(width, slots)]
            + [pl.BlockSpec(memory_space=pl.ANY)] * 3,
            [g_rest] * 3, [jax.ShapeDtypeStruct((width, hid), F32)] * 3, [],
            6 * slots * width * fh, 12 * width * fh, {4: 0, 5: 1, 6: 2},
        )(info_d, h3_rec, pt_turned, qt_turned, gbg, gbu, gad)

        dx_back, a_back, b_back, gbg = tie((dx_back, a_back, b_back, gbg))
        home = (ids_loc // (2 * n_local) == chip)[:, None]
        dx_loc = jnp.where(home, dx_near, dx_back)
        out_loc = jnp.concatenate([jnp.where(home, a_near, a_back), jnp.where(home, b_near, b_back)], 1)

        def rows_last(v, wide):
            return v.reshape(n_local, rank, wide).transpose(0, 2, 1)

        return (out_loc, dx_loc, rows_last(gag, dim), gbg.reshape(n_local, rank, hid), rows_last(gau, dim),
                gbu.reshape(n_local, rank, hid), rows_last(gad, hid), gbd.reshape(n_local, rank, dim))

    return jax.shard_map(
        layer,
        mesh=mesh,
        in_specs=(tok_spec, id_spec, tok_spec, full_spec, full_spec, full_spec, own_spec, own_spec, own_spec, own_spec, own_spec, own_spec),
        out_specs=(tok_spec, tok_spec, grad_spec, grad_spec, grad_spec, grad_spec, grad_spec, grad_spec),
        check_vma=False,
    )
```

time: 2270 us -> 466 us (0.21)
  local copies, waits for them, and re-layouts: 613 us -> 16.8 us
  blocking collectives: 530 us -> 0 us
  matrix products: 318 us -> 0.79 us
  other arithmetic: 175 us -> 5.23 us
  Pallas kernels: 490 us -> 360 us
  waiting for transfers between devices: 89.4 us -> 64.4 us
    all_to_all x5 -> x0, blocking collectives: 530 us -> none  [the longest x3 291 us: to_owner(): arrived = lax.all_to_all(pack_rows(in_rows), 'data', 0, 0, tiled=True)]
    pallas_call x0 -> x13, Pallas kernels: none -> 360 us  [the longest x1 111 us: layer(): call(functools.partial(hidden_kernel, scale, width), (nf,), [const1(slots...]
    gather x22 -> x0, local copies, waits for them, and re-layouts: 342 us -> none  [the longest x5 114 us: to_owner(): return jnp.take(arrived, sort_order, axis=0)]
    another operation x12 -> x0, Pallas kernels: 331 us -> none
    dot_general x6 -> x1, matrix products: 318 us -> 0.79 us  [layer(): ends = jnp.dot(here.astype(F32), before.astype(F32)).astype(jnp.int32)]
    unnamed x59 -> x24, local copies, waits for them, and re-layouts: 268 us -> 8.64 us
    unnamed x8 -> x0, Pallas kernels: 158 us -> none
    all_to_all x6 -> x0, waiting for transfers between devices: 89.4 us -> none  [the longest x3 89.4 us: to_source(): lax.all_to_all(jnp.take(owner_rows, restore, axis=0), 'data', 0, 0, tiled...]
  transfers between devices with their start and end apart: 6 -> 21, of which waited for: 1 -> 9; matrix products, arithmetic and copies ran while one was open for 21% -> 1% of each run, Pallas kernels for 8% -> 48%
where the time goes in v1:
time: 466 us; the launch traced here: 463 us
  Pallas kernels  360 us (77%)
  waiting for transfers between devices  64.4 us (14%)
  local copies, waits for them, and re-layouts  16.8 us (4%)
  starting transfers between devices  14.7 us (3%)
  other arithmetic  5.23 us (1%)
    pallas_call x1, Pallas kernels, layer(): call(functools.partial(hidden_kernel, scale, width), (nf,), [const1(slots...  111 us
    pallas_call x1, Pallas kernels, dx_side(): call(functools.partial(dx_kernel, width), (dim // dt,), [plane(1), plane(...  79.3 us
    pallas_call x2, Pallas kernels, out_side(): call(functools.partial(out_kernel, scale, width), (count,), [plane(0), w_...  48.7 us
    pallas_call x1, Pallas kernels, layer(): call(dh_kernel, (nf,), [const1(slots, dim), w_row, const1(slots, width),...  43.1 us
    ppermute x6, waiting for transfers between devices, chip_swap(): return lax.ppermute(v, 'data', CHIP_SWAP)  39.7 us
    ppermute x15, waiting for transfers between devices, core_swap(): return lax.ppermute(v, 'data', CORE_SWAP)  24.7 us
    pallas_call x2, Pallas kernels, pack(): call(functools.partial(pack_kernel, factor, width, rank, n), (dim // kt,)...  23.1 us
    pallas_call x1, Pallas kernels, layer(): call(functools.partial(wide_grad_kernel, scale, width), (n_half,), [pl.Bl...  19.2 us
  transfers between devices with their start and end apart: 21, of which 9 were waited for; matrix products, arithmetic and copies ran while one was open for 1% of the time, Pallas kernels for 48%

profile of v1, /device:TPU:1, one launch (start us, length us, event | category | flops | bytes accessed | tf_op | source)
XLA Modules:
  0.0 463.4 jit_solution(15061142345790503993)
XLA Ops:
  0.6 0.0 collective-permute-start.2
  0.7 3.2 collective-permute-done.2.r2_ref
  3.9 1.1 copy-done.8
  5.0 2.4 constant_dynamic-slice_fusion
  7.4 1.7 copy-done.1
  9.0 2.0 constant_dynamic-slice_fusion.1
  11.1 2.3 copy-done
  13.3 2.0 constant_dynamic-slice_fusion.2
  15.4 0.1 collective-permute-start.3
  15.5 0.4 collective-permute-start.4
  15.9 0.1 collective-permute-start.5
  16.0 2.6 collective-permute-start
  18.6 1.0 collective-permute-done
  19.5 1.0 collective-permute-start.6
  20.6 0.0 collective-permute-start.8
  20.6 11.4 %collective-permute-done.6 = s32[256]{0:T(256)S(1)} collective-permute-done((s32[256]{0:T(256)S(1)}, s32[256]{0:T(256)S(1)}, u32[]{:S(2)}, u32[]{:S(2)}) %collective-permute-start.6) | collective-permute-done | bytes 1056 | tf_op jit(solution)/shard_map/ppermute | solution.py:245
  32.0 2.3 collective-permute-start.1
  34.4 0.8 fusion.2
  35.9 0.6 select_bitcast_fusion
  36.5 0.6 pad_add_fusion.1.info_ref
  37.0 0.2 select_reduce_fusion
  37.2 26.2 %collective-permute-done.1.r1_ref = bf16[128,5120]{1,0:T(8,128)(2,1)} collective-permute-done((bf16[128,5120]{1,0:T(8,128)(2,1)}, bf16[128,5120]{1,0:T(8,128)(2,1)}, u32[]{:S(2)}, u32[]{:S(2)}) %collective-permute-start.1) | collective-permute-done | bytes 1310752 | tf_op jit(solution)/shard_map/ppermute | solution.py:248
  63.5 0.0 collective-permute-done.3.ads_ref
  63.5 0.0 collective-permute-done.4.bgs_ref
  63.5 1.0 collective-permute-start.9
  64.5 0.9 copy.30.ids_ref
  65.3 2.0 collective-permute-done.9.r3_ref
  67.3 1.1 copy-done.9
  68.4 10.6 %shard_map.179 = (bf16[512,5120]{1,0:T(8,128)(2,1)}, bf16[512,256]{1,0:T(8,128)(2,1)}, bf16[512,256]{1,0:T(8,128)(2,1)}, bf16[256,512]{1,0:T(8,128)(2,1)}, bf16[256,512]{1,0:T(8,128)(2,1)}) custom-call(s32[3]{0:T(128)} %pad_add_fusion.1.info_ref, s32[2,256]{1,0:T(2,128)} %get-tuple-element.83.local_ref, s32[512,1]{1,0:T(8,128)} %copy.30.ids_ref, ...), custom_call_target="tpu_custom_call" | custom-call | flops 2684354560 | bytes 10485760 | tf_op jit(solution)/shard_map/pallas_call | solution.py:290
  79.0 0.4 collective-permute-start.10
  79.4 1.5 collective-permute-start.7
  80.9 0.7 copy-done.4
  81.6 43.1 %shard_map.180.dh_ref = f32[512,6912]{1,0:T(8,128)} custom-call(s32[3]{0:T(128)} %pad_add_fusion.1.info_ref, bf16[512,5120]{1,0:T(8,128)(2,1)} %get-tuple-element.88.dy_ref.base_ref.d_ref, bf16[13824,5120]{1,0:T(8,128)(2,1)} %wd_ref.5, bf16[512,256]{1,0:T(8,128)(2,1)} %get-tuple-element.89.qo_ref, bf16[512,256]{1,0:T(8,128)(2,1)} %copy-done.4, ...), custom_call_target="tpu_custom_call" | custom-call | flops 43486543872 | bytes 70778880 | tf_op jit(solution)/shard_map/pallas_call | solution.py:310
  124.6 0.5 collective-permute-start.11
  125.2 2.9 collective-permute-done.11.r3_ref
  128.1 1.1 copy-done.10
  129.1 12.5 %shard_map.181 = (bf16[512,5120]{1,0:T(8,128)(2,1)}, bf16[512,512]{1,0:T(8,128)(2,1)}, bf16[512,512]{1,0:T(8,128)(2,1)}, bf16[512,512]{1,0:T(8,128)(2,1)}, bf16[512,512]{1,0:T(8,128)(2,1)}) custom-call(s32[3]{0:T(128)} %pad_add_fusion.1.info_ref, s32[2,256]{1,0:T(2,128)} %get-tuple-element.83.local_ref, s32[512,1]{1,0:T(8,128)} %copy.30.ids_ref, ...), custom_call_target="tpu_custom_call" | custom-call | flops 4026531840 | bytes 10485760 | tf_op jit(solution)/shard_map/pallas_call | solution.py:290
  141.6 0.4 collective-permute-start.12
  142.0 1.7 collective-permute-done.12.ps_ref
  143.8 0.8 copy-done.3
  144.5 111.1 %shard_map.182 = (bf16[3,512,6912]{2,1,0:T(8,128)(2,1)}, f32[512,768]{1,0:T(8,128)}, f32[512,768]{1,0:T(8,128)}, f32[256,13824]{1,0:T(8,128)}, f32[256,13824]{1,0:T(8,128)}, /*index=5*/f32[256,13824]{1,0:T(8,128)}) custom-call(s32[3]{0:T(128)} %pad_add_fusion.1.info_ref, bf16[512,5120]{1,0:T(8,128)(2,1)} %get-tuple-element.94.x_ref.base_ref, ...), custom_call_target="tpu_custom_call" | custom-call | flops 86973087744 | bytes 141557760 | tf_op jit(solution)/shard_map/pallas_call | solution.py:322
  255.7 0.4 collective-permute-start.13
  256.1 3.4 collective-permute-done.13.got_ref
  259.5 4.0 shard_map.183
  263.5 0.4 collective-permute-start.20
  263.9 79.3 %shard_map.184 = (f32[256,5120]{1,0:T(8,128)}, f32[256,5120]{1,0:T(8,128)}) custom-call(s32[3]{0:T(128)} %pad_add_fusion.1.info_ref, bf16[3,512,6912]{2,1,0:T(8,128)(2,1)} %get-tuple-element.132.dg_ref.du_ref.h_ref, bf16[3,512,6912]{2,1,0:T(8,128)(2,1)} %get-tuple-element.132.dg_ref.du_ref.h_ref, bf16[5120,13824]{1,0:T(8,128)(2,1)} %wg_ref.3, ...), custom_call_target="tpu_custom_call" | custom-call | flops 72477573120 | bytes 141557760 | tf_op jit(solution)/shard_map/pallas_call | solution.py:353
  343.2 0.0 collective-permute-start.14
  343.2 24.3 %shard_map.185 = (f32[256,2560]{1,0:T(8,128)}, f32[256,2560]{1,0:T(8,128)}) custom-call(s32[3]{0:T(128)} %pad_add_fusion.1.info_ref, bf16[3,512,6912]{2,1,0:T(8,128)(2,1)} %get-tuple-element.132.dg_ref.du_ref.h_ref, bf16[13824,5120]{1,0:T(8,128)(2,1)} %wd_ref.5, bf16[512,768]{1,0:T(8,128)(2,1)} %get-tuple-element.106.q_ref, bf16[256,5120]{1,0:T(8,128)(2,1)} %bitcast.45), custom_call_target="tpu_custom_call" | custom-call | flops 18119393280 | bytes 35389440 | tf_op jit(solution)/shard_map/pallas_call | solution.py:364
  367.6 0.4 collective-permute-start.15
  368.0 0.8 copy.33.local_ref
  368.8 7.9 %shard_map.186 = (bf16[128,5120]{1,0:T(8,128)(2,1)}, bf16[128,5120]{1,0:T(8,128)(2,1)}) custom-call(s32[3]{0:T(128)} %pad_add_fusion.1.info_ref, s32[256,1]{1,0:T(8,128)} %copy.33.local_ref, f32[256,5120]{1,0:T(8,128)} %get-tuple-element.113.mine_ref, f32[256,5120]{1,0:T(8,128)} %collective-permute-done.14.got_ref, ...), custom_call_target="tpu_custom_call" | custom-call | flops 671088640 | bytes 15728640 | tf_op jit(solution)/shard_map/pallas_call | solution.py:375
  376.8 24.4 %shard_map.187 = (f32[256,2560]{1,0:T(8,128)}, f32[256,2560]{1,0:T(8,128)}) custom-call(s32[3]{0:T(128)} %pad_add_fusion.1.info_ref, bf16[3,512,6912]{2,1,0:T(8,128)(2,1)} %get-tuple-element.132.dg_ref.du_ref.h_ref, bf16[13824,5120]{1,0:T(8,128)(2,1)} %wd_ref.5, bf16[512,768]{1,0:T(8,128)(2,1)} %get-tuple-element.106.q_ref, bf16[256,5120]{1,0:T(8,128)(2,1)} %bitcast.46), custom_call_target="tpu_custom_call" | custom-call | flops 18119393280 | bytes 35389440 | tf_op jit(solution)/shard_map/pallas_call | solution.py:364
  401.1 0.1 collective-permute-start.18
  401.2 1.3 collective-permute-start.16
  402.6 5.0 %shard_map.188 = (bf16[128,2560]{1,0:T(8,128)(2,1)}, bf16[128,2560]{1,0:T(8,128)(2,1)}) custom-call(s32[3]{0:T(128)} %pad_add_fusion.1.info_ref, s32[256,1]{1,0:T(8,128)} %copy.33.local_ref, f32[256,2560]{1,0:T(8,128)} %get-tuple-element.109.mine_ref, f32[256,2560]{1,0:T(8,128)} %collective-permute-done.15.got_ref, ...), custom_call_target="tpu_custom_call" | custom-call | flops 335544320 | bytes 7864320 | tf_op jit(solution)/shard_map/pallas_call | solution.py:375
  407.6 0.1 collective-permute-start.17
  407.7 13.7 %shard_map.189 = (f32[256,5120]{1,0:T(8,128)}, f32[256,5120]{1,0:T(8,128)}, f32[256,5120]{1,0:T(8,128)}) custom-call(s32[3]{0:T(128)} %pad_add_fusion.1.info_ref, bf16[512,5120]{1,0:T(8,128)(2,1)} %get-tuple-element.94.x_ref.base_ref, bf16[512,5120]{1,0:T(8,128)(2,1)} %get-tuple-element.88.dy_ref.base_ref.d_ref, bf16[768,512]{1,0:T(8,128)(2,1)} %get-tuple-element.126.qt_ref), custom_call_target="tpu_custom_call" | custom-call | flops 4026531840 | bytes 15728640 | tf_op jit(solution)/shard_map/pallas_call | solution.py:403
  421.4 5.0 %shard_map.190 = (bf16[128,2560]{1,0:T(8,128)(2,1)}, bf16[128,2560]{1,0:T(8,128)(2,1)}) custom-call(s32[3]{0:T(128)} %pad_add_fusion.1.info_ref, s32[256,1]{1,0:T(8,128)} %copy.33.local_ref, f32[256,2560]{1,0:T(8,128)} %get-tuple-element.123.mine_ref, f32[256,2560]{1,0:T(8,128)} %collective-permute-done.18.got_ref, ...), custom_call_target="tpu_custom_call" | custom-call | flops 335544320 | bytes 7864320 | tf_op jit(solution)/shard_map/pallas_call | solution.py:375
  426.4 1.3 collective-permute-start.19
  427.8 0.0 collective-permute-done.20.v_ref
  427.8 19.2 %shard_map.191 = (f32[256,13824]{1,0:T(8,128)}, f32[256,13824]{1,0:T(8,128)}, f32[256,13824]{1,0:T(8,128)}) custom-call(s32[3]{0:T(128)} %pad_add_fusion.1.info_ref, bf16[3,512,6912]{2,1,0:T(8,128)(2,1)} %collective-permute-done.20.v_ref, bf16[512,512]{1,0:T(8,128)(2,1)} %get-tuple-element.133.pt_ref, ...), custom_call_target="tpu_custom_call", output_to_operand_aliasing={{0}: (4, {}), {1}: (5, {}), {2}: (6, {})} | custom-call | flops 5435817984 | bytes 21233664 | tf_op jit(solution)/shard_map/pallas_call | solution.py:417
  447.0 12.5 %collective-permute-done.19 = bf16[128,2560]{1,0:T(8,128)(2,1)} collective-permute-done((bf16[128,2560]{1,0:T(8,128)(2,1)}, bf16[128,2560]{1,0:T(8,128)(2,1)}, u32[]{:S(2)}, u32[]{:S(2)}) %collective-permute-start.19) | collective-permute-done | bytes 655392 | tf_op jit(solution)/shard_map/ppermute | solution.py:248
  459.5 1.9 broadcast_select_fusion.2
  461.4 2.0 pad_maximum_fusion
  (35 shorter events, 0.1 us)
Async XLA Ops:
  0.6 3.3 collective-permute-start.2
  3.9 1.1 copy-start.8
  5.0 4.1 copy-start.1
  9.0 4.3 copy-start
  13.3 2.7 copy-start.6
  15.4 48.1 %collective-permute-start.3 = (bf16[256,6912]{1,0:T(8,128)(2,1)}, bf16[256,6912]{1,0:T(8,128)(2,1)}, u32[]{:S(2)}, u32[]{:S(2)}) collective-permute-start(bf16[256,6912]{1,0:T(8,128)(2,1)} %constant_dynamic-slice_fusion.2), channel_id=1, source_target_pairs={{0,1},{1,0},{2,3},{3,2},{4,5},{5,4},{6,7},{7,6},{8,9},{9,8},{10,11... | collective-permute-start | bytes 10616840 | tf_op jit(solution)/shard_map/ppermute | solution.py:245
  15.5 48.0 %collective-permute-start.4 = (bf16[256,6912]{1,0:T(8,128)(2,1)}, bf16[256,6912]{1,0:T(8,128)(2,1)}, u32[]{:S(2)}, u32[]{:S(2)}) collective-permute-start(bf16[256,6912]{1,0:T(8,128)(2,1)} %constant_dynamic-slice_fusion.1), channel_id=1, source_target_pairs={{0,1},{1,0},{2,3},{3,2},{4,5},{5,4},{6,7},{7,6},{8,9},{9,8},{10,11... | collective-permute-start | bytes 10616840 | tf_op jit(solution)/shard_map/ppermute | solution.py:245
  15.9 47.6 %collective-permute-start.5 = (bf16[256,6912]{1,0:T(8,128)(2,1)S(1)}, bf16[256,6912]{1,0:T(8,128)(2,1)}, u32[]{:S(2)}, u32[]{:S(2)}) collective-permute-start(bf16[256,6912]{1,0:T(8,128)(2,1)S(1)} %constant_dynamic-slice_fusion), channel_id=1, source_target_pairs={{0,1},{1,0},{2,3},{3,2},{4,5},{5,4},{6,7},{7,6},{8,9},{9,8},{10,11... | collective-permute-start | bytes 10616840 | tf_op jit(solution)/shard_map/ppermute | solution.py:245
  16.0 3.5 collective-permute-start
  19.5 12.5 %collective-permute-start.6 = (s32[256]{0:T(256)S(1)}, s32[256]{0:T(256)S(1)}, u32[]{:S(2)}, u32[]{:S(2)}) collective-permute-start(s32[256]{0:T(256)S(1)} %pad_add_fusion), channel_id=1, source_target_pairs={{0,1},{1,0},{2,3},{3,2},{4,5},{5,4},{6,7},{7,6},{8,9},{9,8},{10,11... | collective-permute-start | bytes 3080 | tf_op jit(solution)/shard_map/ppermute | solution.py:245
  20.6 44.8 %collective-permute-start.8 = (bf16[128,5120]{1,0:T(8,128)(2,1)}, bf16[128,5120]{1,0:T(8,128)(2,1)}, u32[]{:S(2)}, u32[]{:S(2)}) collective-permute-start(bf16[128,5120]{1,0:T(8,128)(2,1)} %r0_ref.2), channel_id=1, source_target_pairs={{0,1},{1,0},{2,3},{3,2},{4,5},{5,4},{6,7},{7,6},{8,9},{9,8},{10,11... | collective-permute-start | bytes 3932168 | tf_op jit(solution)/shard_map/ppermute | solution.py:245
  32.0 31.4 %collective-permute-start.1 = (bf16[128,5120]{1,0:T(8,128)(2,1)}, bf16[128,5120]{1,0:T(8,128)(2,1)}, u32[]{:S(2)}, u32[]{:S(2)}) collective-permute-start(bf16[128,5120]{1,0:T(8,128)(2,1)} %r0_ref.2), channel_id=1, source_target_pairs={{0,2},{2,0},{1,3},{3,1},{4,6},{6,4},{5,7},{7,5},{8,10},{10,8},{9,1... | collective-permute-start | bytes 3932168 | tf_op jit(solution)/shard_map/ppermute | solution.py:248
  63.5 3.9 collective-permute-start.9
  67.3 1.1 copy-start.9
  79.0 1.9 collective-permute-start.10
  79.4 45.2 %collective-permute-start.7 = (bf16[128,5120]{1,0:T(8,128)(2,1)}, bf16[128,5120]{1,0:T(8,128)(2,1)}, u32[]{:S(2)}, u32[]{:S(2)}) collective-permute-start(bf16[128,5120]{1,0:T(8,128)(2,1)} %r0_ref.3), channel_id=1, source_target_pairs={{0,2},{2,0},{1,3},{3,1},{4,6},{6,4},{5,7},{7,5},{8,10},{10,8},{9,1... | collective-permute-start | bytes 3932168 | tf_op jit(solution)/shard_map/ppermute | solution.py:248
  80.9 0.7 copy-start.4
  124.6 3.4 collective-permute-start.11
  128.0 1.1 copy-start.10
  141.6 2.2 collective-permute-start.12
  143.7 0.8 copy-start.3
  255.7 3.8 collective-permute-start.13
  263.5 164.2 %collective-permute-start.20 = (bf16[3,512,6912]{2,1,0:T(8,128)(2,1)}, bf16[3,512,6912]{2,1,0:T(8,128)(2,1)}, u32[]{:S(2)}, u32[]{:S(2)}) collective-permute-start(bf16[3,512,6912]{2,1,0:T(8,128)(2,1)} %get-tuple-element.132.dg_ref.du_ref.h_ref), channel_id=1, source_target_pairs={{0,1},{1,0},{2,3},{3,2},{4,5},{5,4},{6,7},{7,6},{8,9},{9,8},{10,11... | collective-permute-start | bytes 63701000 | tf_op jit(solution)/shard_map/ppermute | solution.py:245
  343.2 24.8 %copy-start.5 = (s32[2,256]{1,0:T(2,128)S(1)}, s32[2,256]{1,0:T(2,128)}, u32[]{:S(2)}) copy-start(s32[2,256]{1,0:T(2,128)} %get-tuple-element.83.local_ref) | copy-start | bytes 6148
  343.2 24.4 %collective-permute-start.14 = (f32[256,5120]{1,0:T(8,128)}, f32[256,5120]{1,0:T(8,128)}, u32[]{:S(2)}, u32[]{:S(2)}) collective-permute-start(f32[256,5120]{1,0:T(8,128)} %get-tuple-element.110), channel_id=1, source_target_pairs={{0,1},{1,0},{2,3},{3,2},{4,5},{5,4},{6,7},{7,6},{8,9},{9,8},{10,11... | collective-permute-start | bytes 15728648 | tf_op jit(solution)/shard_map/ppermute | solution.py:245
  367.6 33.5 %collective-permute-start.15 = (f32[256,2560]{1,0:T(8,128)}, f32[256,2560]{1,0:T(8,128)}, u32[]{:S(2)}, u32[]{:S(2)}) collective-permute-start(f32[256,2560]{1,0:T(8,128)} %get-tuple-element.112), channel_id=1, source_target_pairs={{0,1},{1,0},{2,3},{3,2},{4,5},{5,4},{6,7},{7,6},{8,9},{9,8},{10,11... | collective-permute-start | bytes 7864328 | tf_op jit(solution)/shard_map/ppermute | solution.py:245
  401.1 20.3 %collective-permute-start.18 = (f32[256,2560]{1,0:T(8,128)}, f32[256,2560]{1,0:T(8,128)}, u32[]{:S(2)}, u32[]{:S(2)}) collective-permute-start(f32[256,2560]{1,0:T(8,128)} %get-tuple-element.124), channel_id=1, source_target_pairs={{0,1},{1,0},{2,3},{3,2},{4,5},{5,4},{6,7},{7,6},{8,9},{9,8},{10,11... | collective-permute-start | bytes 7864328 | tf_op jit(solution)/shard_map/ppermute | solution.py:245
  401.2 45.8 %collective-permute-start.16 = (bf16[128,5120]{1,0:T(8,128)(2,1)}, bf16[128,5120]{1,0:T(8,128)(2,1)S(1)}, u32[]{:S(2)}, u32[]{:S(2)}) collective-permute-start(bf16[128,5120]{1,0:T(8,128)(2,1)} %get-tuple-element.120), channel_id=1, source_target_pairs={{0,2},{2,0},{1,3},{3,1},{4,6},{6,4},{5,7},{7,5},{8,10},{10,8},{9,1... | collective-permute-start | bytes 3932168 | tf_op jit(solution)/shard_map/ppermute | solution.py:248
  407.6 39.4 %collective-permute-start.17 = (bf16[128,2560]{1,0:T(8,128)(2,1)}, bf16[128,2560]{1,0:T(8,128)(2,1)}, u32[]{:S(2)}, u32[]{:S(2)}) collective-permute-start(bf16[128,2560]{1,0:T(8,128)(2,1)} %get-tuple-element.122), channel_id=1, source_target_pairs={{0,2},{2,0},{1,3},{3,1},{4,6},{6,4},{5,7},{7,5},{8,10},{10,8},{9,1... | collective-permute-start | bytes 1966088 | tf_op jit(solution)/shard_map/ppermute | solution.py:248
  421.4 6.3 %copy-start.7 = (s32[128]{0:T(128)S(1)}, s32[128]{0:T(128)}, u32[]{:S(2)}) copy-start(s32[128]{0:T(128)} %param.13) | copy-start | bytes 1540
  426.4 33.1 %collective-permute-start.19 = (bf16[128,2560]{1,0:T(8,128)(2,1)}, bf16[128,2560]{1,0:T(8,128)(2,1)}, u32[]{:S(2)}, u32[]{:S(2)}) collective-permute-start(bf16[128,2560]{1,0:T(8,128)(2,1)} %get-tuple-element.130), channel_id=1, source_target_pairs={{0,2},{2,0},{1,3},{3,1},{4,6},{6,4},{5,7},{7,5},{8,10},{10,8},{9,1... | collective-permute-start | bytes 1966088 | tf_op jit(solution)/shard_map/ppermute | solution.py:248
  447.0 14.4 %copy-start.2 = (bf16[128,5120]{1,0:T(8,128)(2,1)S(1)}, bf16[128,5120]{1,0:T(8,128)(2,1)}, u32[]{:S(2)}) copy-start(bf16[128,5120]{1,0:T(8,128)(2,1)} %get-tuple-element.142) | copy-start | bytes 3932164

commit v2 on v1

--- a/solution.py
+++ b/solution.py
@@ -105,7 +105,8 @@
 def dh_kernel(info_ref, dy_ref, wd_ref, qo_ref, qs_ref, ado_ref, ads_ref, dh_ref):
     def body(off):
         m = 2 * off
-        eh = (dot_nn(qo_ref[:m], ado_ref[...]) + dot_nn(qs_ref[:m], ads_ref[...])).astype(BF16)
+        ranks = jnp.concatenate([qo_ref[:m], qs_ref[:m]], axis=1)
+        eh = dot_nn(ranks, jnp.concatenate([ado_ref[...], ads_ref[...]], axis=0)).astype(BF16)
         dh_ref[:m] = dot_nt(dy_ref[:m], wd_ref[...]) + eh.astype(F32)
 
     both_forms(info_ref, dy_ref.shape[0] // 2, body)
@@ -125,9 +126,12 @@
     def body(off):
         m = 2 * off
 
+        def both(a, b, axis):
+            return jnp.concatenate([a[...], b[...]], axis=axis)
+
         def rank_side(k, o_ref, s_ref):
             cols = slice(k * width, (k + 1) * width)
-            return dot_nn(po_ref[:m, cols], o_ref[...]) + dot_nn(ps_ref[:m, cols], s_ref[...])
+            return dot_nn(both(po_ref[:m, cols], ps_ref[:m, cols], 1), both(o_ref, s_ref, 0))
 
         eg = (scale * rank_side(0, bgo_ref, bgs_ref)).astype(BF16)
         eu = (scale * rank_side(1, buo_ref, bus_ref)).astype(BF16)
@@ -139,37 +143,40 @@
         h = (act * up).astype(BF16)
         dg = (dh * up * sig * (1.0 + gate * (1.0 - sig))).astype(BF16)
         du = (dh * act).astype(BF16)
+        values = []
         for k, (val, o_ref, s_ref) in enumerate(((h, ado_ref, ads_ref), (dg, bgo_ref, bgs_ref), (du, buo_ref, bus_ref))):
             cols = slice(k * width, (k + 1) * width)
-            h3_ref[k, :m] = val
+            full = val
             if m < slots:
-                h3_ref[k, m:] = jnp.zeros((slots - m, val.shape[1]), BF16)
-            qo_ref[:m, cols] += dot_nt(val, o_ref[...])
-            qs_ref[:m, cols] += dot_nt(val, s_ref[...])
+                full = jnp.concatenate([val, jnp.zeros((slots - m, val.shape[1]), BF16)], axis=0)
+            h3_ref[k] = full
+            values.append(full)
+            sums = dot_nt(val, both(o_ref, s_ref, 0))
+            qo_ref[:m, cols] += sums[:, :width]
+            qs_ref[:m, cols] += sums[:, width:]
+        wide_grads(scale, width, values, pt_ref, qt_ref, gbg_ref, gbu_ref, gad_ref)
 
         @pl.when(step == pl.num_programs(0) - 1)
         def _():
             qs_ref[...] = turned(qs_ref[...], off)
 
     both_forms(info_ref, slots // 2, body)
-    wide_grads(scale, width, h3_ref, pt_ref, qt_ref, gbg_ref, gbu_ref, gad_ref)
-
-
-def wide_grads(scale, width, v_ref, pt_ref, qt_ref, gbg_ref, gbu_ref, gad_ref):
-    gbg_ref[...] = scale * dot_nn(pt_ref[:width, :], v_ref[1])
-    gbu_ref[...] = scale * dot_nn(pt_ref[width:, :], v_ref[2])
-    gad_ref[...] = dot_nn(qt_ref[...], v_ref[0])
+
+
+def wide_grads(scale, width, values, pt_ref, qt_ref, gbg_ref, gbu_ref, gad_ref):
+    h, dg, du = values
+    gbg_ref[...] = scale * dot_nn(pt_ref[:width, :], dg)
+    gbu_ref[...] = scale * dot_nn(pt_ref[width:, :], du)
+    gad_ref[...] = dot_nn(qt_ref[...], h)
 
 
 def rank_kernel(scale, width, rank, info_ref, ids_ref, own_ref, got_ref, q_ref, qt_ref):
     owner = ids_ref[...] - info_ref[0] * (width // rank)
     keep = owner == lax.broadcasted_iota(jnp.int32, (own_ref.shape[0], width), 1) // rank
-    for k in range(3):
-        cols = slice(k * width, (k + 1) * width)
-        total = own_ref[:, cols] + got_ref[:, cols]
-        total = jnp.where(keep, total * scale if k else total, 0.0)
-        q_ref[:, cols] = total.astype(BF16)
-        qt_ref[cols, :] = total.T.astype(BF16)
+    factor = jnp.where(pl.program_id(0) == 0, 1.0, scale)
+    total = jnp.where(keep, (own_ref[...] + got_ref[...]) * factor, 0.0)
+    q_ref[...] = total.astype(BF16)
+    qt_ref[...] = total.T.astype(BF16)
 
 
 def finish_kernel(info_ref, local_ref, mine_ref, got_ref, base_ref, near_ref, far_ref):
@@ -190,8 +197,12 @@
         sib_ref[off:] = rest
 
 
-def dx_kernel(width, info_ref, dg_ref, du_ref, wg_ref, wu_ref, q_ref, ag_ref, au_ref, mine_ref, sib_ref):
+def dx_kernel(scale, width, info_ref, dg_ref, du_ref, wg_ref, wu_ref, q_ref, ag_ref, au_ref, qt_ref, x_ref, d_ref,
+              mine_ref, sib_ref, gbd_ref, gag_ref, gau_ref):
     def body(off):
+        gbd_ref[...] = scale * dot_nn(qt_ref[:width, :], d_ref[...])
+        gag_ref[...] = dot_nn(qt_ref[width:2 * width, :], x_ref[...])
+        gau_ref[...] = dot_nn(qt_ref[2 * width:, :], x_ref[...])
         m = 2 * off
         lora = (dot_nn(q_ref[:m, width:2 * width], ag_ref[...]) + dot_nn(q_ref[:m, 2 * width:], au_ref[...])).astype(BF16)
         tile = dot_nt(dg_ref[0, :m], wg_ref[...]) + dot_nt(du_ref[0, :m], wu_ref[...]) + lora.astype(F32)
@@ -211,13 +222,7 @@
 
 
 def wide_grad_kernel(scale, width, info_ref, v_ref, pt_ref, qt_ref, gbg_in, gbu_in, gad_in, gbg_ref, gbu_ref, gad_ref):
-    wide_grads(scale, width, v_ref, pt_ref, qt_ref, gbg_ref, gbu_ref, gad_ref)
-
-
-def model_grad_kernel(scale, width, info_ref, x_ref, d_ref, qt_ref, gbd_ref, gag_ref, gau_ref):
-    gbd_ref[...] = scale * dot_nn(qt_ref[:width, :], d_ref[...])
-    gag_ref[...] = dot_nn(qt_ref[width:2 * width, :], x_ref[...])
-    gau_ref[...] = dot_nn(qt_ref[2 * width:, :], x_ref[...])
+    wide_grads(scale, width, (v_ref[0], v_ref[1], v_ref[2]), pt_ref, qt_ref, gbg_ref, gbu_ref, gad_ref)
 
 
 def solution(mesh):
@@ -255,9 +260,8 @@
         ad = a_down.transpose(0, 2, 1).reshape(width, hid)
 
         ids_mine = jnp.concatenate([ids_loc, chip_swap(ids_loc)])
-        dy_send, ids_mine = tie((dy_loc, ids_mine))
-        dy1 = chip_swap(dy_send)
-        dy2, x2 = core_swap(dy_send), core_swap(x_loc)
+        dy1 = chip_swap(dy_loc)
+        dy2, x2 = core_swap(dy_loc), core_swap(x_loc)
         late_core, x2 = tie((core, x2))
         ids = jnp.concatenate([ids_mine, core_swap(ids_mine)])
         here = (ids // (2 * n_local) == chip).reshape(2, section)
@@ -281,7 +285,7 @@
         dy3 = core_swap(dy1)
 
         one = dict(pipeline_mode=pl.Buffered(1))
-        kt = 1024
+        kt = 1280
         const = lambda *shape: pl.BlockSpec(shape, lambda i, s: (0,) * len(shape))
         vec = lambda r: pl.BlockSpec((r, kt), lambda i, s: (0, i))
 
@@ -330,10 +334,10 @@
             [], 4 * slots * dim * fh * 1.2, 4 * dim * fh,
         )(info, xc, dh, w_gate, w_up, p_own, core_swap(p_turned), bg, bg_s, bu, bu_s, ad, ad_s, pt_own, qt_own)
 
+        third = pl.BlockSpec((slots, width), lambda i, s: (0, i))
         q, qt = call(
-            functools.partial(rank_kernel, scale, width, rank), (1,),
-            [const(slots, 1), const(slots, 3 * width), const(slots, 3 * width)],
-            [const(slots, 3 * width), const(3 * width, slots)],
+            functools.partial(rank_kernel, scale, width, rank), (3,),
+            [const(slots, 1), third, third], [third, pl.BlockSpec((width, slots), lambda i, s: (i, 0))],
             [jax.ShapeDtypeStruct((slots, 3 * width), BF16), jax.ShapeDtypeStruct((3 * width, slots), BF16)], [],
             1000000, 12 * slots * width,
         )(info, ids_slot[:, None], qo, core_swap(qs))
@@ -347,15 +351,16 @@
             return pl.BlockSpec((1, slots, fh), lambda j, s: (k, 0, 0), **one)
 
         def dx_side(info):
-            w_spec = pl.BlockSpec((dt, fh), lambda j, s: (j, s[1]))
-            l_spec = pl.BlockSpec((width, dt), lambda j, s: (0, j))
-            o_spec = pl.BlockSpec((section, dt), lambda j, s: (0, j))
+            nt = 256
+            w_spec = pl.BlockSpec((nt, fh), lambda j, s: (j, s[1]))
+            tile = lambda r: pl.BlockSpec((r, nt), lambda j, s: (0, j))
             return call(
-                functools.partial(dx_kernel, width), (dim // dt,),
-                [plane(1), plane(2), w_spec, w_spec, q_spec, l_spec, l_spec], [o_spec, o_spec],
-                [jax.ShapeDtypeStruct((section, dim), F32)] * 2, [],
+                functools.partial(dx_kernel, scale, width), (dim // nt,),
+                [plane(1), plane(2), w_spec, w_spec, q_spec, tile(width), tile(width), const1(3 * width, slots), tile(slots), tile(slots)],
+                [tile(section)] * 2 + [tile(width)] * 3,
+                [jax.ShapeDtypeStruct((section, dim), F32)] * 2 + [jax.ShapeDtypeStruct((width, dim), F32)] * 3, [],
                 4 * slots * dim * fh, 4 * dim * fh,
-            )(info, h3, h3, w_gate, w_up, q, ag, au)
+            )(info, h3, h3, w_gate, w_up, q, ag, au, qt, xc, dc)
 
         def out_side(info, first, count):
             w_spec = pl.BlockSpec((fh, dt), lambda j, s: (s[1], first + j))
@@ -382,7 +387,7 @@
 
         n_out = dim // dt // 2
         cut = n_out * dt
-        dx_mine, dx_sib = dx_side(info)
+        dx_mine, dx_sib, gbd, gag, gau = dx_side(info)
         info_a, dx_sib = tie((info, dx_sib))
         dx_got = core_swap(dx_sib)
         a_mine, a_sib = out_side(info_a, 0, n_out)
@@ -395,23 +400,13 @@
         a_got, b_sib = tie((a_got, b_sib))
         a_near, a_far = finish(a_mine, a_got, xc, 0)
         b_got = core_swap(b_sib)
-        info_c, a_far = tie((info, a_far))
         a_back = chip_swap(a_far)
-
-        mt = 640
-        m_spec = lambda r: pl.BlockSpec((r, mt), lambda i, s: (0, i))
-        gbd, gag, gau = call(
-            functools.partial(model_grad_kernel, scale, width), (dim // mt,),
-            [m_spec(slots)] * 2 + [const(3 * width, slots)], [m_spec(width)] * 3,
-            [jax.ShapeDtypeStruct((width, dim), F32)] * 3, [],
-            6 * slots * width * dim, 12 * width * dim,
-        )(info_c, xc, dc, qt)
-        b_got, gbd = tie((b_got, gbd))
+        b_got, a_far = tie((b_got, a_far))
         b_near, b_far = finish(b_mine, b_got, xc, cut)
         info_d, b_far = tie((info, b_far))
         b_back = chip_swap(b_far)
 
-        gt = 768
+        gt = 1152
         n_half = fh // gt
         g_rest = pl.BlockSpec((width, gt), lambda i, s: (0, (1 - s[1]) * n_half + i))
         gbg, gbu, gad = call(

time: 466 us -> 454 us (0.974)
  Pallas kernels: 360 us -> 345 us
  waiting for transfers between devices: 64.4 us -> 72.1 us
    ppermute x6, waiting for transfers between devices: 39.7 us -> 57.6 us  [chip_swap(): return lax.ppermute(v, 'data', CHIP_SWAP)]
    ppermute x15, waiting for transfers between devices: 24.7 us -> 14.5 us  [core_swap(): return lax.ppermute(v, 'data', CORE_SWAP)]
    pallas_call x3 -> x2, Pallas kernels: 97 us -> 88.3 us  [the longest x1 83.7 us: dx_side(): call(functools.partial(dx_kernel, scale, width), (dim // nt,), [plane(1),...]
  transfers between devices with their start and end apart: 21 -> 21, of which waited for: 9 -> 11; matrix products, arithmetic and copies ran while one was open for 1% -> 2% of each run, Pallas kernels for 48% -> 47%
where the time goes in v2:
time: 454 us; the launch traced here: 452 us
  Pallas kernels  345 us (76%)
  waiting for transfers between devices  72.1 us (16%)
  local copies, waits for them, and re-layouts  16.5 us (4%)
  starting transfers between devices  11.2 us (2%)
  other arithmetic  5.27 us (1%)
    pallas_call x1, Pallas kernels, layer(): call(functools.partial(hidden_kernel, scale, width), (nf,), [const1(slots...  107 us
    pallas_call x1, Pallas kernels, dx_side(): call(functools.partial(dx_kernel, scale, width), (dim // nt,), [plane(1),...  83.7 us
    ppermute x6, waiting for transfers between devices, chip_swap(): return lax.ppermute(v, 'data', CHIP_SWAP)  57.6 us
    pallas_call x2, Pallas kernels, out_side(): call(functools.partial(out_kernel, scale, width), (count,), [plane(0), w_...  48.6 us
    pallas_call x1, Pallas kernels, layer(): call(dh_kernel, (nf,), [const1(slots, dim), w_row, const1(slots, width),...  43.1 us
    pallas_call x2, Pallas kernels, pack(): call(functools.partial(pack_kernel, factor, width, rank, n), (dim // kt,)...  22.2 us
    pallas_call x3, Pallas kernels, finish(): call(finish_kernel, (wide // ct,), [const(section, 1), cols(section), col...  18 us
    pallas_call x1, Pallas kernels, layer(): call(functools.partial(wide_grad_kernel, scale, width), (n_half,), [pl.Bl...  17.4 us
  transfers between devices with their start and end apart: 21, of which 11 were waited for; matrix products, arithmetic and copies ran while one was open for 2% of the time, Pallas kernels for 47%

profile of v2, /device:TPU:1, one launch (start us, length us, event | category | flops | bytes accessed | tf_op | source)
XLA Modules:
  0.0 451.8 jit_solution(1785371043964330141)
XLA Ops:
  0.6 0.0 collective-permute-start.1
  0.7 3.2 collective-permute-done.1.r2_ref
  3.9 1.1 copy-done.8
  5.0 2.4 constant_dynamic-slice_fusion.2
  7.4 0.2 collective-permute-start.2
  7.5 1.5 copy-done
  9.0 2.0 constant_dynamic-slice_fusion.1
  11.1 0.1 collective-permute-start.3
  11.2 2.1 copy-done.1
  13.3 2.0 constant_dynamic-slice_fusion
  15.4 0.1 collective-permute-start.4
  15.5 2.6 collective-permute-start
  18.1 0.0 collective-permute-start.5
  18.1 29.3 %collective-permute-done.5 = s32[128]{0:T(128)S(1)} collective-permute-done((s32[128]{0:T(128)S(1)}, s32[128]{0:T(128)S(1)}, u32[]{:S(2)}, u32[]{:S(2)}) %collective-permute-start.5) | collective-permute-done | bytes 544 | tf_op jit(solution)/shard_map/ppermute | solution.py:253
  47.4 0.7 collective-permute-start.6
  48.1 0.8 collective-permute-done.6
  48.9 0.3 collective-permute-start.8
  49.3 0.8 fusion.2
  50.8 0.6 select_bitcast_fusion
  51.4 0.6 pad_add_fusion.1.info_ref
  52.0 0.2 select_reduce_fusion
  52.2 0.0 collective-permute-done.2.ads_ref
  52.2 0.2 collective-permute-start.9
  52.4 0.8 copy.30.ids_ref
  53.3 2.2 collective-permute-done.9.r3_ref
  55.5 1.1 copy-done.9
  56.6 10.3 %shard_map.179 = (bf16[512,5120]{1,0:T(8,128)(2,1)}, bf16[512,256]{1,0:T(8,128)(2,1)}, bf16[512,256]{1,0:T(8,128)(2,1)}, bf16[256,512]{1,0:T(8,128)(2,1)}, bf16[256,512]{1,0:T(8,128)(2,1)}) custom-call(s32[3]{0:T(128)} %pad_add_fusion.1.info_ref, s32[2,256]{1,0:T(2,128)} %get-tuple-element.76.local_ref, s32[512,1]{1,0:T(8,128)} %copy.30.ids_ref, ...), custom_call_target="tpu_custom_call" | custom-call | flops 2684354560 | bytes 10485760 | tf_op jit(solution)/shard_map/pallas_call | solution.py:294
  66.8 0.2 collective-permute-start.10
  67.0 1.5 collective-permute-start.7
  68.5 0.1 collective-permute-done.10.qs_ref
  68.6 0.7 copy-done.4
  69.3 43.1 %shard_map.180.dh_ref = f32[512,6912]{1,0:T(8,128)} custom-call(s32[3]{0:T(128)} %pad_add_fusion.1.info_ref, bf16[512,5120]{1,0:T(8,128)(2,1)} %get-tuple-element.81.dy_ref.d_ref.base_ref, bf16[13824,5120]{1,0:T(8,128)(2,1)} %wd_ref.5, bf16[512,256]{1,0:T(8,128)(2,1)} %get-tuple-element.82.qo_ref, bf16[512,256]{1,0:T(8,128)(2,1)} %copy-done.4, ...), custom_call_target="tpu_custom_call" | custom-call | flops 43486543872 | bytes 70778880 | tf_op jit(solution)/shard_map/pallas_call | solution.py:314
  112.4 0.5 collective-permute-start.11
  112.9 2.9 collective-permute-done.11.r3_ref
  115.8 1.1 copy-done.10
  116.8 11.9 %shard_map.181 = (bf16[512,5120]{1,0:T(8,128)(2,1)}, bf16[512,512]{1,0:T(8,128)(2,1)}, bf16[512,512]{1,0:T(8,128)(2,1)}, bf16[512,512]{1,0:T(8,128)(2,1)}, bf16[512,512]{1,0:T(8,128)(2,1)}) custom-call(s32[3]{0:T(128)} %pad_add_fusion.1.info_ref, s32[2,256]{1,0:T(2,128)} %get-tuple-element.76.local_ref, s32[512,1]{1,0:T(8,128)} %copy.30.ids_ref, ...), custom_call_target="tpu_custom_call" | custom-call | flops 4026531840 | bytes 10485760 | tf_op jit(solution)/shard_map/pallas_call | solution.py:294
  128.8 0.4 collective-permute-start.12
  129.2 1.8 collective-permute-done.12.ps_ref
  130.9 0.8 copy-done.3
  131.7 107.0 %shard_map.182 = (bf16[3,512,6912]{2,1,0:T(8,128)(2,1)}, f32[512,768]{1,0:T(8,128)}, f32[512,768]{1,0:T(8,128)}, f32[256,13824]{1,0:T(8,128)}, f32[256,13824]{1,0:T(8,128)}, /*index=5*/f32[256,13824]{1,0:T(8,128)}) custom-call(s32[3]{0:T(128)} %pad_add_fusion.1.info_ref, bf16[512,5120]{1,0:T(8,128)(2,1)} %get-tuple-element.87.x_ref.base_ref, ...), custom_call_target="tpu_custom_call" | custom-call | flops 86973087744 | bytes 141557760 | tf_op jit(solution)/shard_map/pallas_call | solution.py:326
  238.8 0.3 collective-permute-start.13
  239.1 3.4 collective-permute-done.13.got_ref
  242.5 4.6 %shard_map.183 = (bf16[512,768]{1,0:T(8,128)(2,1)}, bf16[768,512]{1,0:T(8,128)(2,1)}) custom-call(s32[3]{0:T(128)} %pad_add_fusion.1.info_ref, s32[512,1]{1,0:T(8,128)} %copy.30.ids_ref, f32[512,768]{1,0:T(8,128)} %get-tuple-element.96.own_ref, f32[512,768]{1,0:T(8,128)} %collective-permute-done.13.got_ref), custom_call_target="tpu_custom_call" | custom-call | flops 1000000 | bytes 1572864 | tf_op jit(solution)/shard_map/pallas_call | solution.py:338
  247.2 0.3 collective-permute-start.20
  247.5 83.7 %shard_map.184 = (f32[256,5120]{1,0:T(8,128)}, f32[256,5120]{1,0:T(8,128)}, f32[256,5120]{1,0:T(8,128)}, f32[256,5120]{1,0:T(8,128)}, f32[256,5120]{1,0:T(8,128)}) custom-call(s32[3]{0:T(128)} %pad_add_fusion.1.info_ref, bf16[3,512,6912]{2,1,0:T(8,128)(2,1)} %get-tuple-element.122.dg_ref.du_ref.h_ref, ...), custom_call_target="tpu_custom_call" | custom-call | flops 72477573120 | bytes 141557760 | tf_op jit(solution)/shard_map/pallas_call | solution.py:357
  331.2 0.2 collective-permute-start.14
  331.4 24.5 %shard_map.185 = (f32[256,2560]{1,0:T(8,128)}, f32[256,2560]{1,0:T(8,128)}) custom-call(s32[3]{0:T(128)} %pad_add_fusion.1.info_ref, bf16[3,512,6912]{2,1,0:T(8,128)(2,1)} %get-tuple-element.122.dg_ref.du_ref.h_ref, bf16[13824,5120]{1,0:T(8,128)(2,1)} %wd_ref.5, bf16[512,768]{1,0:T(8,128)(2,1)} %get-tuple-element.99.q_ref, bf16[256,5120]{1,0:T(8,128)(2,1)} %bitcast.45), custom_call_target="tpu_custom_call" | custom-call | flops 18119393280 | bytes 35389440 | tf_op jit(solution)/shard_map/pallas_call | solution.py:369
  355.9 0.2 collective-permute-start.15
  356.2 0.8 copy.33.local_ref
  357.0 8.0 %shard_map.186 = (bf16[128,5120]{1,0:T(8,128)(2,1)}, bf16[128,5120]{1,0:T(8,128)(2,1)}) custom-call(s32[3]{0:T(128)} %pad_add_fusion.1.info_ref, s32[256,1]{1,0:T(8,128)} %copy.33.local_ref, f32[256,5120]{1,0:T(8,128)} %get-tuple-element.107.mine_ref, f32[256,5120]{1,0:T(8,128)} %collective-permute-done.14.got_ref, ...), custom_call_target="tpu_custom_call" | custom-call | flops 671088640 | bytes 15728640 | tf_op jit(solution)/shard_map/pallas_call | solution.py:380
  364.9 24.1 %shard_map.187 = (f32[256,2560]{1,0:T(8,128)}, f32[256,2560]{1,0:T(8,128)}) custom-call(s32[3]{0:T(128)} %pad_add_fusion.1.info_ref, bf16[3,512,6912]{2,1,0:T(8,128)(2,1)} %get-tuple-element.122.dg_ref.du_ref.h_ref, bf16[13824,5120]{1,0:T(8,128)(2,1)} %wd_ref.5, bf16[512,768]{1,0:T(8,128)(2,1)} %get-tuple-element.99.q_ref, bf16[256,5120]{1,0:T(8,128)(2,1)} %bitcast.46), custom_call_target="tpu_custom_call" | custom-call | flops 18119393280 | bytes 35389440 | tf_op jit(solution)/shard_map/pallas_call | solution.py:369
  389.0 0.4 collective-permute-start.18
  389.4 1.4 collective-permute-start.16
  390.7 5.1 %shard_map.188 = (bf16[128,2560]{1,0:T(8,128)(2,1)}, bf16[128,2560]{1,0:T(8,128)(2,1)}) custom-call(s32[3]{0:T(128)} %pad_add_fusion.1.info_ref, s32[256,1]{1,0:T(8,128)} %copy.33.local_ref, f32[256,2560]{1,0:T(8,128)} %get-tuple-element.103.mine_ref, f32[256,2560]{1,0:T(8,128)} %collective-permute-done.15.got_ref, ...), custom_call_target="tpu_custom_call" | custom-call | flops 335544320 | bytes 7864320 | tf_op jit(solution)/shard_map/pallas_call | solution.py:380
  395.8 0.1 collective-permute-start.17
  395.9 5.0 %shard_map.189 = (bf16[128,2560]{1,0:T(8,128)(2,1)}, bf16[128,2560]{1,0:T(8,128)(2,1)}) custom-call(s32[3]{0:T(128)} %pad_add_fusion.1.info_ref, s32[256,1]{1,0:T(8,128)} %copy.33.local_ref, f32[256,2560]{1,0:T(8,128)} %get-tuple-element.116.mine_ref, f32[256,2560]{1,0:T(8,128)} %collective-permute-done.18.got_ref, ...), custom_call_target="tpu_custom_call" | custom-call | flops 335544320 | bytes 7864320 | tf_op jit(solution)/shard_map/pallas_call | solution.py:380
  400.9 1.4 collective-permute-start.19
  402.3 0.0 collective-permute-done.20.v_ref
  402.3 17.4 %shard_map.190 = (f32[256,13824]{1,0:T(8,128)}, f32[256,13824]{1,0:T(8,128)}, f32[256,13824]{1,0:T(8,128)}) custom-call(s32[3]{0:T(128)} %pad_add_fusion.1.info_ref, bf16[3,512,6912]{2,1,0:T(8,128)(2,1)} %collective-permute-done.20.v_ref, bf16[512,512]{1,0:T(8,128)(2,1)} %get-tuple-element.123.pt_ref, ...), custom_call_target="tpu_custom_call", output_to_operand_aliasing={{0}: (4, {}), {1}: (5, {}), {2}: (6, {})} | custom-call | flops 5435817984 | bytes 21233664 | tf_op jit(solution)/shard_map/pallas_call | solution.py:412
  419.7 0.1 collective-permute-done.16
  419.8 14.1 %collective-permute-done.17 = bf16[128,2560]{1,0:T(8,128)(2,1)} collective-permute-done((bf16[128,2560]{1,0:T(8,128)(2,1)}, bf16[128,2560]{1,0:T(8,128)(2,1)}, u32[]{:S(2)}, u32[]{:S(2)}) %collective-permute-start.17) | collective-permute-done | bytes 655392 | tf_op jit(solution)/shard_map/ppermute | solution.py:253
  433.9 14.0 %collective-permute-done.19 = bf16[128,2560]{1,0:T(8,128)(2,1)} collective-permute-done((bf16[128,2560]{1,0:T(8,128)(2,1)}, bf16[128,2560]{1,0:T(8,128)(2,1)}, u32[]{:S(2)}, u32[]{:S(2)}) %collective-permute-start.19) | collective-permute-done | bytes 655392 | tf_op jit(solution)/shard_map/ppermute | solution.py:253
  448.0 1.9 broadcast_select_fusion.2
  449.8 2.0 pad_maximum_fusion
  (35 shorter events, 0.1 us)
Async XLA Ops:
  0.6 3.3 collective-permute-start.1
  3.9 1.1 copy-start.8
  5.0 4.1 copy-start
  7.4 44.8 %collective-permute-start.2 = (bf16[256,6912]{1,0:T(8,128)(2,1)S(1)}, bf16[256,6912]{1,0:T(8,128)(2,1)}, u32[]{:S(2)}, u32[]{:S(2)}) collective-permute-start(bf16[256,6912]{1,0:T(8,128)(2,1)S(1)} %constant_dynamic-slice_fusion.2), channel_id=1, source_target_pairs={{0,1},{1,0},{2,3},{3,2},{4,5},{5,4},{6,7},{7,6},{8,9},{9,8},{10,11... | collective-permute-start | bytes 10616840 | tf_op jit(solution)/shard_map/ppermute | solution.py:250
  9.0 4.3 copy-start.1
  11.1 41.1 %collective-permute-start.3 = (bf16[256,6912]{1,0:T(8,128)(2,1)}, bf16[256,6912]{1,0:T(8,128)(2,1)}, u32[]{:S(2)}, u32[]{:S(2)}) collective-permute-start(bf16[256,6912]{1,0:T(8,128)(2,1)} %constant_dynamic-slice_fusion.1), channel_id=1, source_target_pairs={{0,1},{1,0},{2,3},{3,2},{4,5},{5,4},{6,7},{7,6},{8,9},{9,8},{10,11... | collective-permute-start | bytes 10616840 | tf_op jit(solution)/shard_map/ppermute | solution.py:250
  13.3 4.7 %copy-start.6 = (s32[128]{0:T(128)S(1)}, s32[128]{0:T(128)}, u32[]{:S(2)}) copy-start(s32[128]{0:T(128)} %param.13) | copy-start | bytes 1540
  15.4 36.9 %collective-permute-start.4 = (bf16[256,6912]{1,0:T(8,128)(2,1)}, bf16[256,6912]{1,0:T(8,128)(2,1)}, u32[]{:S(2)}, u32[]{:S(2)}) collective-permute-start(bf16[256,6912]{1,0:T(8,128)(2,1)} %constant_dynamic-slice_fusion), channel_id=1, source_target_pairs={{0,1},{1,0},{2,3},{3,2},{4,5},{5,4},{6,7},{7,6},{8,9},{9,8},{10,11... | collective-permute-start | bytes 10616840 | tf_op jit(solution)/shard_map/ppermute | solution.py:250
  15.5 36.7 %collective-permute-start = (bf16[128,5120]{1,0:T(8,128)(2,1)}, bf16[128,5120]{1,0:T(8,128)(2,1)}, u32[]{:S(2)}, u32[]{:S(2)}) collective-permute-start(bf16[128,5120]{1,0:T(8,128)(2,1)} %r0_ref.2), channel_id=1, source_target_pairs={{0,2},{2,0},{1,3},{3,1},{4,6},{6,4},{5,7},{7,5},{8,10},{10,8},{9,1... | collective-permute-start | bytes 3932168 | tf_op jit(solution)/shard_map/ppermute | solution.py:253
  18.1 29.3 %collective-permute-start.5 = (s32[128]{0:T(128)S(1)}, s32[128]{0:T(128)S(1)}, u32[]{:S(2)}, u32[]{:S(2)}) collective-permute-start(s32[128]{0:T(128)S(1)} %copy-done.6), channel_id=1, source_target_pairs={{0,2},{2,0},{1,3},{3,1},{4,6},{6,4},{5,7},{7,5},{8,10},{10,8},{9,1... | collective-permute-start | bytes 1544 | tf_op jit(solution)/shard_map/ppermute | solution.py:253
  47.4 1.5 collective-permute-start.6
  48.9 4.3 collective-permute-start.8
  52.2 3.3 collective-permute-start.9
  55.5 1.1 copy-start.9
  66.8 1.8 collective-permute-start.10
  67.0 45.4 %collective-permute-start.7 = (bf16[128,5120]{1,0:T(8,128)(2,1)}, bf16[128,5120]{1,0:T(8,128)(2,1)}, u32[]{:S(2)}, u32[]{:S(2)}) collective-permute-start(bf16[128,5120]{1,0:T(8,128)(2,1)} %r0_ref.3), channel_id=1, source_target_pairs={{0,2},{2,0},{1,3},{3,1},{4,6},{6,4},{5,7},{7,5},{8,10},{10,8},{9,1... | collective-permute-start | bytes 3932168 | tf_op jit(solution)/shard_map/ppermute | solution.py:253
  68.6 0.7 copy-start.4
  112.4 3.3 collective-permute-start.11
  115.8 1.1 copy-start.10
  128.8 2.2 collective-permute-start.12
  130.9 0.8 copy-start.3
  238.8 3.8 collective-permute-start.13
  247.2 155.1 %collective-permute-start.20 = (bf16[3,512,6912]{2,1,0:T(8,128)(2,1)}, bf16[3,512,6912]{2,1,0:T(8,128)(2,1)}, u32[]{:S(2)}, u32[]{:S(2)}) collective-permute-start(bf16[3,512,6912]{2,1,0:T(8,128)(2,1)} %get-tuple-element.122.dg_ref.du_ref.h_ref), channel_id=1, source_target_pairs={{0,1},{1,0},{2,3},{3,2},{4,5},{5,4},{6,7},{7,6},{8,9},{9,8},{10,11... | collective-permute-start | bytes 63701000 | tf_op jit(solution)/shard_map/ppermute | solution.py:250
  331.1 25.0 %copy-start.5 = (s32[2,256]{1,0:T(2,128)S(1)}, s32[2,256]{1,0:T(2,128)}, u32[]{:S(2)}) copy-start(s32[2,256]{1,0:T(2,128)} %get-tuple-element.76.local_ref) | copy-start | bytes 6148
  331.2 24.8 %collective-permute-start.14 = (f32[256,5120]{1,0:T(8,128)}, f32[256,5120]{1,0:T(8,128)}, u32[]{:S(2)}, u32[]{:S(2)}) collective-permute-start(f32[256,5120]{1,0:T(8,128)} %get-tuple-element.104), channel_id=1, source_target_pairs={{0,1},{1,0},{2,3},{3,2},{4,5},{5,4},{6,7},{7,6},{8,9},{9,8},{10,11... | collective-permute-start | bytes 15728648 | tf_op jit(solution)/shard_map/ppermute | solution.py:250
  355.9 33.1 %collective-permute-start.15 = (f32[256,2560]{1,0:T(8,128)}, f32[256,2560]{1,0:T(8,128)}, u32[]{:S(2)}, u32[]{:S(2)}) collective-permute-start(f32[256,2560]{1,0:T(8,128)} %get-tuple-element.106), channel_id=1, source_target_pairs={{0,1},{1,0},{2,3},{3,2},{4,5},{5,4},{6,7},{7,6},{8,9},{9,8},{10,11... | collective-permute-start | bytes 7864328 | tf_op jit(solution)/shard_map/ppermute | solution.py:250
  389.0 6.9 %collective-permute-start.18 = (f32[256,2560]{1,0:T(8,128)}, f32[256,2560]{1,0:T(8,128)}, u32[]{:S(2)}, u32[]{:S(2)}) collective-permute-start(f32[256,2560]{1,0:T(8,128)} %get-tuple-element.117), channel_id=1, source_target_pairs={{0,1},{1,0},{2,3},{3,2},{4,5},{5,4},{6,7},{7,6},{8,9},{9,8},{10,11... | collective-permute-start | bytes 7864328 | tf_op jit(solution)/shard_map/ppermute | solution.py:250
  389.4 30.4 %collective-permute-start.16 = (bf16[128,5120]{1,0:T(8,128)(2,1)}, bf16[128,5120]{1,0:T(8,128)(2,1)S(1)}, u32[]{:S(2)}, u32[]{:S(2)}) collective-permute-start(bf16[128,5120]{1,0:T(8,128)(2,1)} %get-tuple-element.114), channel_id=1, source_target_pairs={{0,2},{2,0},{1,3},{3,1},{4,6},{6,4},{5,7},{7,5},{8,10},{10,8},{9,1... | collective-permute-start | bytes 3932168 | tf_op jit(solution)/shard_map/ppermute | solution.py:253
  395.8 38.1 %collective-permute-start.17 = (bf16[128,2560]{1,0:T(8,128)(2,1)}, bf16[128,2560]{1,0:T(8,128)(2,1)}, u32[]{:S(2)}, u32[]{:S(2)}) collective-permute-start(bf16[128,2560]{1,0:T(8,128)(2,1)} %get-tuple-element.115), channel_id=1, source_target_pairs={{0,2},{2,0},{1,3},{3,1},{4,6},{6,4},{5,7},{7,5},{8,10},{10,8},{9,1... | collective-permute-start | bytes 1966088 | tf_op jit(solution)/shard_map/ppermute | solution.py:253
  395.9 6.3 %copy-start.7 = (s32[128]{0:T(128)S(1)}, s32[128]{0:T(128)}, u32[]{:S(2)}) copy-start(s32[128]{0:T(128)} %param.13) | copy-start | bytes 1540
  400.9 47.1 %collective-permute-start.19 = (bf16[128,2560]{1,0:T(8,128)(2,1)}, bf16[128,2560]{1,0:T(8,128)(2,1)}, u32[]{:S(2)}, u32[]{:S(2)}) collective-permute-start(bf16[128,2560]{1,0:T(8,128)(2,1)} %get-tuple-element.120), channel_id=1, source_target_pairs={{0,2},{2,0},{1,3},{3,1},{4,6},{6,4},{5,7},{7,5},{8,10},{10,8},{9,1... | collective-permute-start | bytes 1966088 | tf_op jit(solution)/shard_map/ppermute | solution.py:253
  419.7 30.2 %copy-start.2 = (bf16[128,5120]{1,0:T(8,128)(2,1)S(1)}, bf16[128,5120]{1,0:T(8,128)(2,1)}, u32[]{:S(2)}) copy-start(bf16[128,5120]{1,0:T(8,128)(2,1)} %get-tuple-element.132) | copy-start | bytes 3932164
